TPU v7x, 32 devices: a whole 2x2x4 slice. The times are simulated.
32 devices in a mesh: dp: 16 (over z, y, core), fsdp: 2 (over x).
Axes of the slice: x: 2, y: 2, z: 4, core: 2. Of those that a mesh axis runs over, the one named last changes fastest.
Arguments:
- patches: bfloat16 [16384, 768], P(('dp', 'fsdp')), may hold values from -6 to 6
- cotangent: bfloat16 [16384, 768], P(('dp', 'fsdp')), may hold values from -6 to 6
- lengths: int32 [32, 4], P(('dp', 'fsdp')), may hold values from 0 to 512, as said below
- arrange: int32 [16384], P(('dp', 'fsdp')), may hold values from 0 to 511, as said below
- first_gain: bfloat16 [768], P('dp'), may hold values from 0.3984375 to 1.59375
- first_shift: bfloat16 [768], P('dp'), may hold values from -1.5 to 1.5
- project_weight: bfloat16 [768, 2304], P('dp', 'fsdp'), may hold values from -0.21875 to 0.21875
- query_bias: bfloat16 [768], P('dp'), may hold values from -1.5 to 1.5
- value_bias: bfloat16 [768], P('dp'), may hold values from -1.5 to 1.5
- output_weight: bfloat16 [768, 768], P('dp', 'fsdp'), may hold values from -1.75 to 1.75
- output_bias: bfloat16 [768], P('dp'), may hold values from -1.5 to 1.5
- second_gain: bfloat16 [768], P('dp'), may hold values from 0.3984375 to 1.59375
- second_shift: bfloat16 [768], P('dp'), may hold values from -1.5 to 1.5
- up_weight: bfloat16 [768, 3072], P('dp', 'fsdp'), may hold values from -0.21875 to 0.21875
- up_bias: bfloat16 [3072], P('dp'), may hold values from -1.5 to 1.5
- down_weight: bfloat16 [3072, 768], P('dp', 'fsdp'), may hold values from -0.109375 to 0.109375
- down_bias: bfloat16 [768], P('dp'), may hold values from -1.5 to 1.5
Outputs:
- encoded: bfloat16 [16384, 768], P(('dp', 'fsdp'))
- grad_patches: bfloat16 [16384, 768], P(('dp', 'fsdp'))
- grad_first_gain: float32 [768], P('dp')
- grad_first_shift: float32 [768], P('dp')
- grad_project_weight: float32 [768, 2304], P('dp', 'fsdp')
- grad_query_bias: float32 [768], P('dp')
- grad_value_bias: float32 [768], P('dp')
- grad_output_weight: float32 [768, 768], P('dp', 'fsdp')
- grad_output_bias: float32 [768], P('dp')
- grad_second_gain: float32 [768], P('dp')
- grad_second_shift: float32 [768], P('dp')
- grad_up_weight: float32 [768, 3072], P('dp', 'fsdp')
- grad_up_bias: float32 [3072], P('dp')
- grad_down_weight: float32 [3072, 768], P('dp', 'fsdp')
- grad_down_bias: float32 [768], P('dp')
Inputs may be any that keep to these rules, and one draw needn't show every extreme that they name: Each block's 4 lengths sum to at least 384 and at most 512; slots may be empty; in every draw some block holds a single sequence of 512 rows. `arrange`: each block's 512 entries are a permutation of 0 to 511.
All inputs are finite; a program needn't handle non-finite values.
Results may differ from a plain program's by a relative error of at most 0.012.
Values may be sent and summed in bfloat16 or wider, within the bound.
A program may use at most 128 MiB of HBM per device.

v0:
```python
import jax
import jax.numpy as jnp
from jax import lax
from jax.sharding import PartitionSpec as P

HEADS = 12
HEAD = 64


NORM_EPSILON = 1e-12
MASK_VALUE = -1e30
ROOT_HALF = 0.7071067811865476


def norm_rows(values, norm_gain, norm_shift):
    center = values - jnp.mean(values, axis=-1, keepdims=True)
    spread = jnp.mean(center * center, axis=-1, keepdims=True)
    return center * lax.rsqrt(spread + NORM_EPSILON) * norm_gain + norm_shift


def gelu_exact(values):
    return 0.5 * values * (1.0 + lax.erf(values * ROOT_HALF))


def slot_labels(lengths, arrange):
    total_rows = arrange.shape[0]
    slot_ends = jnp.cumsum(lengths[0])
    position = jnp.arange(total_rows, dtype=jnp.int32)
    slot_index = jnp.sum((position[:, None] >= slot_ends[None, :]).astype(jnp.int32), axis=1)
    return jnp.zeros((total_rows,), jnp.int32).at[arrange].set(slot_index)


def matmul(left_side, right_side, pattern):
    return jnp.einsum(pattern, left_side, right_side, preferred_element_type=jnp.float32)


def column_sums(values):
    return jnp.sum(values.astype(jnp.float32), axis=0)


def local(
    patches,
    cotangent,
    lengths,
    arrange,
    first_gain,
    first_shift,
    project_weight,
    query_bias,
    value_bias,
    output_weight,
    output_bias,
    second_gain,
    second_shift,
    up_weight,
    up_bias,
    down_weight,
    down_bias,
):
    arrived, cot_rows = (
        lax.all_to_all(patches, "dp", split_axis=0, concat_axis=0, tiled=True),
        lax.all_to_all(cotangent, "dp", split_axis=0, concat_axis=0, tiled=True),
    )
    total_rows, width = patches.shape
    labels = slot_labels(lengths, arrange)
    live_rows = (labels < lengths.shape[1]).astype(jnp.float32)[:, None]
    project_part, output_part, up_part, down_part = (
        lax.all_gather(project_weight, "fsdp", axis=1, tiled=True),
        lax.all_gather(output_weight, "fsdp", axis=1, tiled=True),
        lax.all_gather(up_weight, "fsdp", axis=1, tiled=True),
        lax.all_gather(down_weight, "fsdp", axis=1, tiled=True),
    )
    attn_set = (
        lax.all_gather(first_gain, "dp", axis=0, tiled=True),
        lax.all_gather(first_shift, "dp", axis=0, tiled=True),
        lax.all_gather(project_part, "dp", axis=0, tiled=True),
        lax.all_gather(query_bias, "dp", axis=0, tiled=True),
        lax.all_gather(value_bias, "dp", axis=0, tiled=True),
        lax.all_gather(output_part, "dp", axis=0, tiled=True),
        lax.all_gather(output_bias, "dp", axis=0, tiled=True),
    )
    inputs = arrived.astype(jnp.float32)
    gain_one = attn_set[0].astype(jnp.float32)
    shift_one = attn_set[1].astype(jnp.float32)
    normed_one = norm_rows(inputs, gain_one, shift_one)
    normed_low = normed_one.astype(jnp.bfloat16)
    joint = jnp.dot(normed_low, attn_set[2], preferred_element_type=jnp.float32)
    queries = (
        (joint[:, :width] + attn_set[3].astype(jnp.float32))
        .astype(jnp.bfloat16)
        .reshape(total_rows, HEADS, HEAD)
    )
    key_rows = joint[:, width : 2 * width].astype(jnp.bfloat16).reshape(total_rows, HEADS, HEAD)
    value_rows = (
        (joint[:, 2 * width :] + attn_set[4].astype(jnp.float32))
        .astype(jnp.bfloat16)
        .reshape(total_rows, HEADS, HEAD)
    )
    score_scale = HEAD ** (-0.5)
    block_rows = min(512, total_rows)
    block_starts = jnp.arange(total_rows // block_rows, dtype=jnp.int32) * block_rows

    def block_scores():
        raw_scores = matmul(queries, key_rows, "qhe,khe->hqk") * score_scale
        visible = labels[:, None] == labels[None, :]
        return (queries, jnp.where(visible[None], raw_scores, MASK_VALUE))

    def attend(start):
        query_block, scores = block_scores()
        top_score = jnp.max(scores, axis=-1, keepdims=True)
        weights = jnp.exp(scores - top_score)
        totals = jnp.sum(weights, axis=-1, keepdims=True)
        prob_low = (weights / totals).astype(jnp.bfloat16)
        mixed_rows = matmul(prob_low, value_rows, "hqk,khe->qhe")
        return (mixed_rows.astype(jnp.bfloat16), (top_score + jnp.log(totals))[:, :, 0])

    mixed_blocks, log_totals = lax.map(attend, block_starts)
    attended = mixed_blocks.reshape(total_rows, width)
    attn_out = jnp.dot(attended, attn_set[5], preferred_element_type=jnp.float32) + attn_set[
        6
    ].astype(jnp.float32)
    hidden = inputs + attn_out
    mlp_set = (
        lax.all_gather(second_gain, "dp", axis=0, tiled=True),
        lax.all_gather(second_shift, "dp", axis=0, tiled=True),
        lax.all_gather(up_part, "dp", axis=0, tiled=True),
        lax.all_gather(up_bias, "dp", axis=0, tiled=True),
        lax.all_gather(down_part, "dp", axis=0, tiled=True),
        lax.all_gather(down_bias, "dp", axis=0, tiled=True),
    )
    gain_two = mlp_set[0].astype(jnp.float32)
    shift_two = mlp_set[1].astype(jnp.float32)
    normed_two = norm_rows(hidden, gain_two, shift_two)
    normed_two_low = normed_two.astype(jnp.bfloat16)
    pre_act = jnp.dot(normed_two_low, mlp_set[2], preferred_element_type=jnp.float32) + mlp_set[
        3
    ].astype(jnp.float32)
    activated = gelu_exact(pre_act).astype(jnp.bfloat16)
    branch = jnp.dot(activated, mlp_set[4], preferred_element_type=jnp.float32) + mlp_set[5].astype(
        jnp.float32
    )
    encoded_rows = live_rows * (hidden + branch)
    grad_out = live_rows * cot_rows.astype(jnp.float32)
    grad_branch = grad_out.astype(jnp.bfloat16)
    again_two = (
        lax.all_gather(second_gain, "dp", axis=0, tiled=True),
        lax.all_gather(second_shift, "dp", axis=0, tiled=True),
        lax.all_gather(up_part, "dp", axis=0, tiled=True),
        lax.all_gather(up_bias, "dp", axis=0, tiled=True),
        lax.all_gather(down_part, "dp", axis=0, tiled=True),
        lax.all_gather(down_bias, "dp", axis=0, tiled=True),
    )
    grad_down = matmul(activated, grad_branch, "tf,td->fd")
    grad_downbias = column_sums(grad_branch)
    grad_activ = matmul(grad_branch, again_two[4], "td,fd->tf")
    grad_pre = jax.vjp(gelu_exact, pre_act)[1](grad_activ)[0].astype(jnp.bfloat16)
    grad_up = matmul(normed_two_low, grad_pre, "td,tf->df")
    grad_upbias = column_sums(grad_pre)
    grad_normed_two = matmul(grad_pre, again_two[2], "tf,df->td")
    norm_pull_two = jax.vjp(
        norm_rows, hidden, again_two[0].astype(jnp.float32), again_two[1].astype(jnp.float32)
    )[1]
    grad_hidden_part, grad_gain_two, grad_shift_two = norm_pull_two(grad_normed_two)
    grad_hidden = grad_out + grad_hidden_part
    mlp_sums = (
        lax.psum_scatter(grad_up, "dp", scatter_dimension=0, tiled=True),
        lax.psum_scatter(grad_down, "dp", scatter_dimension=0, tiled=True),
        lax.psum_scatter(grad_gain_two, "dp", scatter_dimension=0, tiled=True),
        lax.psum_scatter(grad_shift_two, "dp", scatter_dimension=0, tiled=True),
        lax.psum_scatter(grad_upbias, "dp", scatter_dimension=0, tiled=True),
        lax.psum_scatter(grad_downbias, "dp", scatter_dimension=0, tiled=True),
    )
    again_one = (
        lax.all_gather(first_gain, "dp", axis=0, tiled=True),
        lax.all_gather(first_shift, "dp", axis=0, tiled=True),
        lax.all_gather(project_part, "dp", axis=0, tiled=True),
        lax.all_gather(query_bias, "dp", axis=0, tiled=True),
        lax.all_gather(value_bias, "dp", axis=0, tiled=True),
        lax.all_gather(output_part, "dp", axis=0, tiled=True),
        lax.all_gather(output_bias, "dp", axis=0, tiled=True),
    )
    grad_attn = grad_hidden.astype(jnp.bfloat16)
    grad_output = matmul(attended, grad_attn, "td,te->de")
    grad_outbias = column_sums(grad_attn)
    grad_attended = (
        matmul(grad_attn, again_one[5], "te,de->td")
        .astype(jnp.bfloat16)
        .reshape(total_rows, HEADS, HEAD)
    )

    def back_block(carry, block_item):
        key_acc, value_acc = carry
        start, log_block = block_item
        query_block, scores = block_scores()
        prob_full = jnp.exp(scores - log_block[:, :, None])
        prob_low = prob_full.astype(jnp.bfloat16)
        value_acc = value_acc + matmul(prob_low, grad_attended, "hqk,qhe->khe")
        grad_prob = matmul(grad_attended, value_rows, "qhe,khe->hqk")
        inner = jnp.sum(prob_full * grad_prob, axis=-1, keepdims=True)
        grad_scores = (prob_full * (grad_prob - inner)).astype(jnp.bfloat16)
        query_grad = matmul(grad_scores, key_rows, "hqk,khe->qhe") * score_scale
        key_acc = key_acc + matmul(grad_scores, query_block, "hqk,qhe->khe") * score_scale
        return ((key_acc, value_acc), query_grad.astype(jnp.bfloat16))

    zero_acc = jnp.zeros((total_rows, HEADS, HEAD), jnp.float32)
    (key_grad_sum, value_grad_sum), query_grads = lax.scan(
        back_block, (zero_acc, zero_acc), (block_starts, log_totals)
    )
    grad_queries = query_grads.reshape(total_rows, width)
    grad_keys = key_grad_sum.reshape(total_rows, width).astype(jnp.bfloat16)
    grad_values = value_grad_sum.reshape(total_rows, width).astype(jnp.bfloat16)
    grad_joint = jnp.concatenate([grad_queries, grad_keys, grad_values], axis=1)
    grad_project = matmul(normed_low, grad_joint, "td,tf->df")
    grad_querybias = column_sums(grad_queries)
    grad_valuebias = column_sums(grad_values)
    grad_normed_one = matmul(grad_joint, again_one[2], "tf,df->td")
    norm_pull_one = jax.vjp(
        norm_rows, inputs, again_one[0].astype(jnp.float32), again_one[1].astype(jnp.float32)
    )[1]
    grad_input_part, grad_gain_one, grad_shift_one = norm_pull_one(grad_normed_one)
    grad_inputs = grad_hidden + grad_input_part
    attn_sums = (
        lax.psum_scatter(grad_project, "dp", scatter_dimension=0, tiled=True),
        lax.psum_scatter(grad_output, "dp", scatter_dimension=0, tiled=True),
        lax.psum_scatter(grad_gain_one, "dp", scatter_dimension=0, tiled=True),
        lax.psum_scatter(grad_shift_one, "dp", scatter_dimension=0, tiled=True),
        lax.psum_scatter(grad_querybias, "dp", scatter_dimension=0, tiled=True),
        lax.psum_scatter(grad_valuebias, "dp", scatter_dimension=0, tiled=True),
        lax.psum_scatter(grad_outbias, "dp", scatter_dimension=0, tiled=True),
    )
    matrix_parts = (
        lax.psum_scatter(
            attn_sums[0].astype(jnp.bfloat16), "fsdp", scatter_dimension=1, tiled=True
        ).astype(jnp.float32),
        lax.psum_scatter(
            attn_sums[1].astype(jnp.bfloat16), "fsdp", scatter_dimension=1, tiled=True
        ).astype(jnp.float32),
        lax.psum_scatter(
            mlp_sums[0].astype(jnp.bfloat16), "fsdp", scatter_dimension=1, tiled=True
        ).astype(jnp.float32),
        lax.psum_scatter(
            mlp_sums[1].astype(jnp.bfloat16), "fsdp", scatter_dimension=1, tiled=True
        ).astype(jnp.float32),
    )
    vector_parts = lax.psum(
        (
            attn_sums[2],
            attn_sums[3],
            attn_sums[4],
            attn_sums[5],
            attn_sums[6],
            mlp_sums[2],
            mlp_sums[3],
            mlp_sums[4],
            mlp_sums[5],
        ),
        "fsdp",
    )
    encoded_back, grad_back = (
        lax.all_to_all(
            encoded_rows.astype(jnp.bfloat16), "dp", split_axis=0, concat_axis=0, tiled=True
        ),
        lax.all_to_all(
            grad_inputs.astype(jnp.bfloat16), "dp", split_axis=0, concat_axis=0, tiled=True
        ),
    )
    return (
        encoded_back,
        grad_back,
        vector_parts[0],
        vector_parts[1],
        matrix_parts[0],
        vector_parts[2],
        vector_parts[3],
        matrix_parts[1],
        vector_parts[4],
        vector_parts[5],
        vector_parts[6],
        matrix_parts[2],
        vector_parts[7],
        matrix_parts[3],
        vector_parts[8],
    )


def solution(mesh):
    return jax.shard_map(
        local,
        mesh=mesh,
        in_specs=(
            P(("dp", "fsdp"), None),
            P(("dp", "fsdp"), None),
            P(("dp", "fsdp"), None),
            P(("dp", "fsdp")),
            P("dp"),
            P("dp"),
            P("dp", "fsdp"),
            P("dp"),
            P("dp"),
            P("dp", "fsdp"),
            P("dp"),
            P("dp"),
            P("dp"),
            P("dp", "fsdp"),
            P("dp"),
            P("dp", "fsdp"),
            P("dp"),
        ),
        out_specs=(
            P(("dp", "fsdp"), None),
            P(("dp", "fsdp"), None),
            P("dp"),
            P("dp"),
            P("dp", "fsdp"),
            P("dp"),
            P("dp"),
            P("dp", "fsdp"),
            P("dp"),
            P("dp"),
            P("dp"),
            P("dp", "fsdp"),
            P("dp"),
            P("dp", "fsdp"),
            P("dp"),
        ),
        check_vma=False,
    )
```

profile of v0, /device:TPU:0, one launch (start us, length us, event | category | flops | bytes accessed | tf_op | source)
XLA Modules:
  0.0 716.0 jit_solution(9440607187867650082)
XLA Ops:
  7.2 8.7 %all_gather.59 = bf16[48,2304]{1,0:T(8,128)(2,1)} all-gather(bf16[48,1152]{1,0:T(8,128)(2,1)} %param.23), channel_id=1, replica_groups=mesh['dp'=16,'fsdp'=2] {'fsdp'}, dimensions={1}, use_global_device_ids=true | all-gather | bytes 331776 | tf_op jit(solution)/shard_map/all_gather | solution.py:68
  16.0 4.9 all_gather.63
  21.1 7.0 all_gather.68
  28.2 6.0 all-to-all-start
  34.2 6.9 all_gather.71
  41.4 14.7 %all-to-all-done = bf16[16,32,768]{2,1,0:T(8,128)(2,1)S(1)} async-done(((bf16[16,32,768]{2,1,0:T(8,128)(2,1)}), bf16[16,32,768]{2,1,0:T(8,128)(2,1)S(1)}, u32[]{:S(2)}, u32[]{:S(2)}) %all-to-all-start) | async-done | bytes 786464 | tf_op jit(solution)/shard_map/all_to_all | solution.py:61
  56.1 14.3 %all-to-all-start.2 = ((bf16[16,32,768]{2,1,0:T(8,128)(2,1)}), bf16[16,32,768]{2,1,0:T(8,128)(2,1)S(1)}, u32[]{:S(2)}, u32[]{:S(2)}) async-start(bf16[16,32,768]{2,1,0:T(8,128)(2,1)} %bitcast.13), calls=%async_computation.2 | async-start | bytes 1572864 | tf_op jit(solution)/shard_map/all_to_all | solution.py:62
  74.6 66.2 %all-reduce.20 = (bf16[768]{0:T(1024)(128)(2,1)S(1)}, bf16[768]{0:T(1024)(128)(2,1)S(1)}, bf16[768]{0:T(1024)(128)(2,1)S(1)}, bf16[768]{0:T(1024)(128)(2,1)S(1)}...) all-reduce(bf16[768]{0:T(1024)(128)(2,1)S(1)} %dynamic-update-slice, ...), channel_id=1, replica_groups=mesh['dp'=16,'fsdp'=2] {'dp'}, use_global_device_ids=true, to_apply=%add.1 | all-reduce | flops 9216 | bytes 36864
  164.2 4.6 fusion.24
  171.6 7.2 %fusion.39 = f32[512,3072]{1,0:T(8,128)} fusion(bf16[768,3072]{1,0:T(8,128)(2,1)} %all-gather.9.cloned.1.call-done, f32[512,768]{1,0:T(8,128)S(1)} %get-tuple-element.114, f32[768]{0:T(1024)} %convert_element_type.197, f32[768]{0:T(1024)S(1)} %convert_element_type.196, f32[512]{0:T(512)S(1)} %fusion.28, f32[512]{0:T(512)S(1)} %broadcast_multiply_fusion.1), kind=kOutput, calls=%fused_computation.87 | convolution fusion | flops 2417885184 | bytes 12593152 | tf_op jit(solution)/shard_map/dot_general | solution.py:135
  178.8 41.9 %all-gather.11.cloned.1.call-done = bf16[3072,768]{1,0:T(8,128)(2,1)} async-done(((bf16[192,768]{1,0:T(8,128)(2,1)}), bf16[3072,768]{1,0:T(8,128)(2,1)}) %all-gather.11.cloned.1.call-update) | async-done | bytes 4718608 | tf_op jit(solution)/shard_map/all_gather | solution.py:128
  220.7 9.5 %convert_reduce_fusion = (f32[3072]{0:T(1024)S(1)}, bf16[512,3072]{1,0:T(8,128)(2,1)S(1)}, bf16[512,3072]{1,0:T(8,128)(2,1)}) fusion(f32[512,3072]{1,0:T(8,128)} %fusion.39, f32[3072]{0:T(1024)S(1)} %convert_element_type.199, bf16[512,768]{1,0:T(8,128)(2,1)} %fusion.20, bf16[3072,768]{1,0:T(8,128)(2,1)} %all-gather.11.cloned.1.call-done), kind=kOutput, calls=%fused_computation.10 | convolution fusion | flops 2444227584 | bytes 18112512 | tf_op jit(solution)/shard_map/td,fd->tf/dot_general | solution.py:34
  244.9 13.8 %multiply_reduce_fusion = (f32[12,512]{1,0:T(8,128)S(1)}, f32[12,512,512]{1,2,0:T(8,128)}) fusion(f32[12,512]{1,0:T(8,128)S(1)} %log_add_fusion, f32[12,512,512]{1,2,0:T(8,128)} %copy-done, pred[512,512]{0,1:T(8,128)(4,1)S(1)} %broadcast_compare_fusion, bf16[512,12,64]{0,2,1:T(8,128)(2,1)} %bitcast.111, bf16[512,12,64]{0,2,1:T(8,128)(2,1)} %bitcast.109), kind=kOutput, calls=%fused_computation.2 | convolution fusion | flops 418375680 | bytes 27049984 | tf_op jit(solution)/shard_map/while/body/eval_jaxpr/qhe,khe->hqk/dot_general | solution.py:34
  258.7 7.2 %multiply_convert_fusion = bf16[12,512,512]{1,2,0:T(8,128)(2,1)S(1)} fusion(f32[12,512,512]{1,2,0:T(8,128)} %get-tuple-element.117, f32[12,512]{1,0:T(8,128)S(1)} %get-tuple-element.116, f32[12,512]{1,0:T(8,128)S(1)} %log_add_fusion, f32[12,512,512]{1,2,0:T(8,128)S(1)} %bitcast.104, pred[512,512]{0,1:T(8,128)(4,1)S(1)} %broadcast_compare_fusion), kind=kLoop, calls=%fused_computation.1 | loop fusion | flops 18874368 | bytes 31768576 | tf_op jit(solution)/shard_map/while/body/eval_jaxpr/convert_element_type | solution.py:200
  274.3 4.9 fusion.25
  279.5 8.4 %fusion.47 = f32[3072,768]{1,0:T(8,128)} fusion(bf16[512,3072]{1,0:T(8,128)(2,1)} %get-tuple-element.106, bf16[512,768]{1,0:T(8,128)(2,1)} %fusion.20), kind=kOutput, calls=%fused_computation.94 | convolution fusion | flops 2415919104 | bytes 13369344 | tf_op jit(solution)/shard_map/tf,td->fd/dot_general | solution.py:34
  288.6 8.9 %fusion.38 = f32[768,3072]{1,0:T(8,128)} fusion(bf16[512,3072]{1,0:T(8,128)(2,1)} %copy-done.32, f32[512,768]{1,0:T(8,128)} %copy-done.5, f32[768]{0:T(1024)S(1)} %copy-done.16, f32[768]{0:T(1024)S(1)} %convert_element_type.196, f32[512]{0:T(512)S(1)} %fusion.28, f32[512]{0:T(512)S(1)} %broadcast_multiply_fusion.1), kind=kOutput, calls=%fused_computation.86 | convolution fusion | flops 2417885184 | bytes 14166016 | tf_op jit(solution)/shard_map/td,tf->df/dot_general | solution.py:34
  298.2 7.2 %multiply_convert_fusion.5 = bf16[512,768]{1,0:T(8,128)(2,1)} fusion(f32[512,768]{1,0:T(8,128)} %copy-done.5, bf16[512,3072]{1,0:T(8,128)(2,1)} %get-tuple-element.106, bf16[3072,768]{1,0:T(8,128)(2,1)} %all-gather.11.cloned.1.call-done, f32[768]{0:T(1024)S(1)} %convert_element_type.201, f32[512]{0:T(512)S(1)} %compare_convert_fusion), kind=kOutput, calls=%fused_computation.52 | convolution fusion | flops 2417491968 | bytes 10228736 | tf_op jit(solution)/shard_map/dot_general | solution.py:139
  309.7 5.0 fusion.40
  318.6 80.5 %reduce-scatter.15.cloned.1.call-done = f32[48,2304]{1,0:T(8,128)} async-done(((f32[768,2304]{1,0:T(8,128)}), f32[48,2304]{1,0:T(8,128)}) %reduce-scatter.15.cloned.1.call-update) | async-done | bytes 442384 | tf_op jit(solution)/shard_map/reduce_scatter | solution.py:223
  408.4 105.7 %reduce-scatter.23.cloned.1.call-done = f32[192,768]{1,0:T(8,128)} async-done(((f32[3072,768]{1,0:T(8,128)}), f32[192,768]{1,0:T(8,128)}) %reduce-scatter.23.cloned.1.call-update) | async-done | bytes 589840 | tf_op jit(solution)/shard_map/reduce_scatter | solution.py:167
  516.2 112.9 %reduce-scatter.19.cloned.1.call-done = f32[48,3072]{1,0:T(8,128)} async-done(((f32[768,3072]{1,0:T(8,128)}), f32[48,3072]{1,0:T(8,128)}) %reduce-scatter.19.cloned.1.call-update) | async-done | bytes 589840 | tf_op jit(solution)/shard_map/reduce_scatter | solution.py:166
  632.6 60.3 %all-reduce.18 = (f32[768]{0:T(1024)S(1)}, f32[768]{0:T(1024)S(1)}, f32[768]{0:T(1024)S(1)}, f32[768]{0:T(1024)S(1)}, f32[768]{0:T(1024)S(1)}, /*index=5*/f32[76...) all-reduce(f32[768]{0:T(1024)S(1)} %get-tuple-element.68, ...), channel_id=2, replica_groups=mesh['dp'=16,'fsdp'=2] {'dp'}, use_global_device_ids=true, to_apply=%region_15.16.clone | all-reduce | flops 9216 | bytes 73728
  693.6 5.5 all-reduce.19
  (210 shorter events, 86.0 us)
Async XLA Ops:
  7.2 139.3 %all-gather.5.cloned.1.call-start = ((), (), s32[]{:S(2)}) async-start(), calls=%async_computation.12 | async-start | bytes 3760128 | tf_op jit(solution)/shard_map/all_gather | solution.py:76
  15.9 152.8 %all-gather.7.cloned.1.call-start = ((), (), s32[]{:S(2)}) async-start(), calls=%async_computation.13 | async-start | bytes 1253376 | tf_op jit(solution)/shard_map/all_gather | solution.py:79
  21.0 52.2 %copy-start.25 = (bf16[48]{0:T(256)(128)(2,1)S(1)}, bf16[48]{0:T(256)(128)(2,1)}, u32[]{:S(2)}) copy-start(bf16[48]{0:T(256)(128)(2,1)} %param.24) | copy-start | bytes 292
  21.0 52.4 %copy-start.26 = (bf16[48]{0:T(256)(128)(2,1)S(1)}, bf16[48]{0:T(256)(128)(2,1)}, u32[]{:S(2)}) copy-start(bf16[48]{0:T(256)(128)(2,1)} %param.25) | copy-start | bytes 292
  21.0 52.6 %copy-start.27 = (bf16[48]{0:T(256)(128)(2,1)S(1)}, bf16[48]{0:T(256)(128)(2,1)}, u32[]{:S(2)}) copy-start(bf16[48]{0:T(256)(128)(2,1)} %param.21) | copy-start | bytes 292
  21.0 52.8 %copy-start.28 = (bf16[48]{0:T(256)(128)(2,1)S(1)}, bf16[48]{0:T(256)(128)(2,1)}, u32[]{:S(2)}) copy-start(bf16[48]{0:T(256)(128)(2,1)} %param.22) | copy-start | bytes 292
  21.0 53.0 %copy-start.29 = (bf16[48]{0:T(256)(128)(2,1)S(1)}, bf16[48]{0:T(256)(128)(2,1)}, u32[]{:S(2)}) copy-start(bf16[48]{0:T(256)(128)(2,1)} %param.33) | copy-start | bytes 292
  21.0 53.3 %copy-start.30 = (bf16[192]{0:T(256)(128)(2,1)S(1)}, bf16[192]{0:T(256)(128)(2,1)}, u32[]{:S(2)}) copy-start(bf16[192]{0:T(256)(128)(2,1)} %param.31) | copy-start | bytes 1156
  21.1 120.3 %copy-start.19 = (s32[512]{0:T(512)S(1)}, s32[512]{0:T(512)}, u32[]{:S(2)}) copy-start(s32[512]{0:T(512)} %param.20) | copy-start | bytes 6148
  21.1 150.5 %all-gather.9.cloned.1.call-start = ((), (), s32[]{:S(2)}) async-start(), calls=%async_computation.14 | async-start | bytes 5013504 | tf_op jit(solution)/shard_map/all_gather | solution.py:126
  28.2 27.9 %all-to-all-start = ((bf16[16,32,768]{2,1,0:T(8,128)(2,1)}), bf16[16,32,768]{2,1,0:T(8,128)(2,1)S(1)}, u32[]{:S(2)}, u32[]{:S(2)}) async-start(bf16[16,32,768]{2,1,0:T(8,128)(2,1)} %bitcast.119), calls=%async_computation | async-start | bytes 1572864 | tf_op jit(solution)/shard_map/all_to_all | solution.py:61
  34.1 186.6 %all-gather.11.cloned.1.call-start = ((), (), s32[]{:S(2)}) async-start(), calls=%async_computation.15 | async-start | bytes 5013504 | tf_op jit(solution)/shard_map/all_gather | solution.py:128
  56.1 88.9 %all-to-all-start.2 = ((bf16[16,32,768]{2,1,0:T(8,128)(2,1)}), bf16[16,32,768]{2,1,0:T(8,128)(2,1)S(1)}, u32[]{:S(2)}, u32[]{:S(2)}) async-start(bf16[16,32,768]{2,1,0:T(8,128)(2,1)} %bitcast.13), calls=%async_computation.2 | async-start | bytes 1572864 | tf_op jit(solution)/shard_map/all_to_all | solution.py:62
  70.4 246.4 %reduce-scatter.17.cloned.1.call-start = ((), (), s32[]{:S(2)}) async-start(), calls=%async_computation.17 | async-start | bytes 2506752 | tf_op jit(solution)/shard_map/reduce_scatter | solution.py:224
  171.2 59.0 %copy-start.5 = (f32[512,768]{1,0:T(8,128)}, f32[512,768]{1,0:T(8,128)S(1)}, u32[]{:S(2)}) copy-start(f32[512,768]{1,0:T(8,128)S(1)} %get-tuple-element.114) | copy-start | bytes 4718596
  244.3 154.8 %reduce-scatter.15.cloned.1.call-start = ((), (), s32[]{:S(2)}) async-start(), calls=%async_computation.16 | async-start | bytes 7520256 | tf_op jit(solution)/shard_map/reduce_scatter | solution.py:223
  279.2 234.8 %reduce-scatter.23.cloned.1.call-start = ((), (), s32[]{:S(2)}) async-start(), calls=%async_computation.20 | async-start | bytes 10027008 | tf_op jit(solution)/shard_map/reduce_scatter | solution.py:167
  287.9 341.1 %reduce-scatter.19.cloned.1.call-start = ((), (), s32[]{:S(2)}) async-start(), calls=%async_computation.18 | async-start | bytes 10027008 | tf_op jit(solution)/shard_map/reduce_scatter | solution.py:166
  305.4 98.6 %all-to-all-start.1 = ((bf16[16,32,768]{2,1,0:T(8,128)(2,1)}), bf16[16,32,768]{2,1,0:T(8,128)(2,1)}, u32[]{:S(2)}, u32[]{:S(2)}) async-start(bf16[16,32,768]{2,1,0:T(8,128)(2,1)} %bitcast.120), calls=%async_computation.1 | async-start | bytes 1572864 | tf_op jit(solution)/shard_map/all_to_all | solution.py:260
  309.7 389.4 %reduce-scatter.27.cloned.1.call-start = ((), (), s32[]{:S(2)}) async-start(), calls=%async_computation.22 | async-start | bytes 294912
  318.6 382.2 %reduce-scatter.25.cloned.1.call-start = ((), (), s32[]{:S(2)}) async-start(), calls=%async_computation.21 | async-start | bytes 884736
  404.0 295.1 %all-to-all-start.3 = ((bf16[16,32,768]{2,1,0:T(8,128)(2,1)}), bf16[16,32,768]{2,1,0:T(8,128)(2,1)S(1)}, u32[]{:S(2)}, u32[]{:S(2)}) async-start(bf16[16,32,768]{2,1,0:T(8,128)(2,1)} %bitcast.114), calls=%async_computation.3 | async-start | bytes 1572864 | tf_op jit(solution)/shard_map/all_to_all | solution.py:263
  408.4 294.2 %reduce-scatter.29.cloned.1.call-start = ((), (), s32[]{:S(2)}) async-start(), calls=%async_computation.23 | async-start | bytes 589824
  516.1 188.3 %reduce-scatter.21.cloned.1.call-start = ((), (), s32[]{:S(2)}) async-start(), calls=%async_computation.19 | async-start | bytes 442368 | tf_op jit(solution)/shard_map/reduce_scatter | solution.py:238
  (28 other events, 373.1 us)
Sparse Core Ops, SparseCore 0:
  16.0 54.1 all-gather.4
  72.6 39.9 all-gather.6
  114.8 51.9 all-gather.8
  169.0 51.6 all-gather.10
  244.4 61.8 reduce-scatter.16
  310.1 88.9 reduce-scatter.14
  403.2 110.8 reduce-scatter.22
  518.2 110.8 reduce-scatter.18
  631.8 10.7 reduce-scatter.26
  644.7 15.3 reduce-scatter.24
  662.9 13.1 reduce-scatter.28
  678.8 12.1 reduce-scatter.20
where the time goes:
time: 722 us; the launch traced here: 716 us
  waiting for transfers between devices  356 us (49%)
  blocking collectives  160 us (22%)
  matrix products  94.3 us (13%)
  starting transfers between devices  30 us (4%)
  local copies, waits for them, and re-layouts  29.4 us (4%)
  other arithmetic  29.1 us (4%)
  between operations  17.6 us (2%)
    unnamed x2, blocking collectives  126 us
    reduce_scatter x1, waiting for transfers between devices, local(): lax.psum_scatter(grad_up, 'dp', scatter_dimension=0, tiled=True)  113 us
    reduce_scatter x1, waiting for transfers between devices, local(): lax.psum_scatter(grad_down, 'dp', scatter_dimension=0, tiled=True)  106 us
    reduce_scatter x1, waiting for transfers between devices, local(): lax.psum_scatter(grad_project, 'dp', scatter_dimension=0, tiled=True)  80.5 us
    dot_general x14, matrix products, matmul(): jnp.einsum(pattern, left_side, right_side, preferred_element_type=jnp.flo...  73.1 us
    all_gather x1, waiting for transfers between devices, local(): lax.all_gather(down_part, 'dp', axis=0, tiled=True)  41.9 us
    unnamed x108, local copies, waits for them, and re-layouts  18.6 us
    all_to_all x1, waiting for transfers between devices, local(): lax.all_to_all(patches, 'dp', split_axis=0, concat_axis=0, tiled=True)  14.7 us
  transfers between devices with their start and end apart: 16, of which 5 were waited for; matrix products, arithmetic and copies ran while one was open for 17% of the time, Pallas kernels for 0%

commit v1 on v0

v1 whole, which is shorter than its diff:
```python
import jax
import jax.numpy as jnp
from jax import lax
from jax.sharding import PartitionSpec as P

HEADS = 12
HEAD = 64


NORM_EPSILON = 1e-12
MASK_VALUE = -1e30
ROOT_HALF = 0.7071067811865476


def norm_rows(values, norm_gain, norm_shift):
    center = values - jnp.mean(values, axis=-1, keepdims=True)
    spread = jnp.mean(center * center, axis=-1, keepdims=True)
    return center * lax.rsqrt(spread + NORM_EPSILON) * norm_gain + norm_shift


def gelu_exact(values):
    return 0.5 * values * (1.0 + lax.erf(values * ROOT_HALF))


def slot_labels(lengths, arrange):
    total_rows = arrange.shape[0]
    slot_ends = jnp.cumsum(lengths[0])
    position = jnp.arange(total_rows, dtype=jnp.int32)
    slot_index = jnp.sum((position[:, None] >= slot_ends[None, :]).astype(jnp.int32), axis=1)
    return jnp.zeros((total_rows,), jnp.int32).at[arrange].set(slot_index)


def matmul(left_side, right_side, pattern):
    return jnp.einsum(pattern, left_side, right_side, preferred_element_type=jnp.float32)


def column_sums(values):
    return jnp.sum(values.astype(jnp.float32), axis=0)


def gather_matrix(block, n_dp, n_fsdp):
    rows, cols = block.shape
    every = lax.all_gather(block, ("dp", "fsdp"), axis=0, tiled=False)
    every = every.reshape(n_dp, n_fsdp, rows, cols).transpose(0, 2, 1, 3)
    return every.reshape(n_dp * rows, n_fsdp * cols)


def scatter_matrix(grad):
    part = lax.psum_scatter(grad.astype(jnp.bfloat16), "dp", scatter_dimension=0, tiled=True)
    part = lax.psum_scatter(part, "fsdp", scatter_dimension=1, tiled=True)
    return part.astype(jnp.float32)


def local(
    n_dp,
    n_fsdp,
    patches,
    cotangent,
    lengths,
    arrange,
    first_gain,
    first_shift,
    project_weight,
    query_bias,
    value_bias,
    output_weight,
    output_bias,
    second_gain,
    second_shift,
    up_weight,
    up_bias,
    down_weight,
    down_bias,
):
    arrived, cot_rows = (
        lax.all_to_all(patches, "dp", split_axis=0, concat_axis=0, tiled=True),
        lax.all_to_all(cotangent, "dp", split_axis=0, concat_axis=0, tiled=True),
    )
    total_rows, width = patches.shape
    labels = slot_labels(lengths, arrange)
    live_rows = (labels < lengths.shape[1]).astype(jnp.float32)[:, None]

    vector_parts = (
        first_gain, first_shift, query_bias, value_bias, output_bias,
        second_gain, second_shift, up_bias, down_bias,
    )
    widths = [v.shape[0] for v in vector_parts]
    packed = lax.all_gather(jnp.concatenate(vector_parts)[None], "dp", axis=0, tiled=True)
    vectors = []
    offset = 0
    for w in widths:
        vectors.append(packed[:, offset : offset + w].reshape(-1).astype(jnp.float32))
        offset += w
    gain_one, shift_one, query_full, value_full, outbias_full, gain_two, shift_two, upbias_full, downbias_full = vectors

    project_full = gather_matrix(project_weight, n_dp, n_fsdp)
    output_full = gather_matrix(output_weight, n_dp, n_fsdp)
    up_full = gather_matrix(up_weight, n_dp, n_fsdp)
    down_full = gather_matrix(down_weight, n_dp, n_fsdp)

    inputs = arrived.astype(jnp.float32)
    normed_one = norm_rows(inputs, gain_one, shift_one)
    normed_low = normed_one.astype(jnp.bfloat16)
    joint = jnp.dot(normed_low, project_full, preferred_element_type=jnp.float32)
    queries = (
        (joint[:, :width] + query_full).astype(jnp.bfloat16).reshape(total_rows, HEADS, HEAD)
    )
    key_rows = joint[:, width : 2 * width].astype(jnp.bfloat16).reshape(total_rows, HEADS, HEAD)
    value_rows = (
        (joint[:, 2 * width :] + value_full).astype(jnp.bfloat16).reshape(total_rows, HEADS, HEAD)
    )
    score_scale = HEAD ** (-0.5)
    visible = labels[:, None] == labels[None, :]

    def block_scores():
        raw_scores = matmul(queries, key_rows, "qhe,khe->hqk") * score_scale
        return jnp.where(visible[None], raw_scores, MASK_VALUE)

    scores = block_scores()
    top_score = jnp.max(scores, axis=-1, keepdims=True)
    weights = jnp.exp(scores - top_score)
    totals = jnp.sum(weights, axis=-1, keepdims=True)
    prob_low = (weights / totals).astype(jnp.bfloat16)
    mixed_rows = matmul(prob_low, value_rows, "hqk,khe->qhe")
    log_totals = top_score + jnp.log(totals)
    attended = mixed_rows.astype(jnp.bfloat16).reshape(total_rows, width)
    attn_out = jnp.dot(attended, output_full, preferred_element_type=jnp.float32) + outbias_full
    hidden = inputs + attn_out
    normed_two = norm_rows(hidden, gain_two, shift_two)
    normed_two_low = normed_two.astype(jnp.bfloat16)
    pre_act = jnp.dot(normed_two_low, up_full, preferred_element_type=jnp.float32) + upbias_full
    activated = gelu_exact(pre_act).astype(jnp.bfloat16)
    branch = jnp.dot(activated, down_full, preferred_element_type=jnp.float32) + downbias_full
    encoded_rows = live_rows * (hidden + branch)
    encoded_back = lax.all_to_all(
        encoded_rows.astype(jnp.bfloat16), "dp", split_axis=0, concat_axis=0, tiled=True
    )

    grad_out = live_rows * cot_rows.astype(jnp.float32)
    grad_branch = grad_out.astype(jnp.bfloat16)
    grad_down = matmul(activated, grad_branch, "tf,td->fd")
    grad_downbias = column_sums(grad_branch)
    grad_activ = matmul(grad_branch, down_full, "td,fd->tf")
    grad_pre = jax.vjp(gelu_exact, pre_act)[1](grad_activ)[0].astype(jnp.bfloat16)
    grad_up = matmul(normed_two_low, grad_pre, "td,tf->df")
    grad_upbias = column_sums(grad_pre)
    grad_normed_two = matmul(grad_pre, up_full, "tf,df->td")
    norm_pull_two = jax.vjp(norm_rows, hidden, gain_two, shift_two)[1]
    grad_hidden_part, grad_gain_two, grad_shift_two = norm_pull_two(grad_normed_two)
    grad_hidden = grad_out + grad_hidden_part
    down_low, up_low = grad_down.astype(jnp.bfloat16), grad_up.astype(jnp.bfloat16)
    grad_hidden, down_low, up_low = lax.optimization_barrier((grad_hidden, down_low, up_low))
    down_part = scatter_matrix(down_low)
    up_part = scatter_matrix(up_low)

    grad_attn = grad_hidden.astype(jnp.bfloat16)
    grad_output = matmul(attended, grad_attn, "td,te->de")
    grad_outbias = column_sums(grad_attn)
    grad_attended = (
        matmul(grad_attn, output_full, "te,de->td").astype(jnp.bfloat16).reshape(total_rows, HEADS, HEAD)
    )
    output_low = grad_output.astype(jnp.bfloat16)
    grad_attended, output_low = lax.optimization_barrier((grad_attended, output_low))
    output_part = scatter_matrix(output_low)

    scores = block_scores()
    prob_full = jnp.exp(scores - log_totals)
    prob_low = prob_full.astype(jnp.bfloat16)
    value_grad = matmul(prob_low, grad_attended, "hqk,qhe->khe")
    grad_prob = matmul(grad_attended, value_rows, "qhe,khe->hqk")
    inner = jnp.sum(prob_full * grad_prob, axis=-1, keepdims=True)
    grad_scores = (prob_full * (grad_prob - inner)).astype(jnp.bfloat16)
    query_grad = matmul(grad_scores, key_rows, "hqk,khe->qhe") * score_scale
    key_grad = matmul(grad_scores, queries, "hqk,qhe->khe") * score_scale
    grad_queries = query_grad.astype(jnp.bfloat16).reshape(total_rows, width)
    grad_keys = key_grad.reshape(total_rows, width).astype(jnp.bfloat16)
    grad_values = value_grad.reshape(total_rows, width).astype(jnp.bfloat16)
    grad_joint = jnp.concatenate([grad_queries, grad_keys, grad_values], axis=1)
    grad_project = matmul(normed_low, grad_joint, "td,tf->df")
    grad_querybias = column_sums(grad_queries)
    grad_valuebias = column_sums(grad_values)
    project_part = scatter_matrix(grad_project)
    grad_normed_one = matmul(grad_joint, project_full, "tf,df->td")
    norm_pull_one = jax.vjp(norm_rows, inputs, gain_one, shift_one)[1]
    grad_input_part, grad_gain_one, grad_shift_one = norm_pull_one(grad_normed_one)
    grad_inputs = grad_hidden + grad_input_part
    grad_back = lax.all_to_all(
        grad_inputs.astype(jnp.bfloat16), "dp", split_axis=0, concat_axis=0, tiled=True
    )

    vector_grads = (
        grad_gain_one, grad_shift_one, grad_querybias, grad_valuebias, grad_outbias,
        grad_gain_two, grad_shift_two, grad_upbias, grad_downbias,
    )
    stacked = jnp.concatenate([g.reshape(n_dp, -1) for g in vector_grads], axis=1)
    stacked = stacked + lax.ppermute(stacked, "fsdp", [(i, (i + 1) % n_fsdp) for i in range(n_fsdp)])
    mine = lax.psum_scatter(stacked, "dp", scatter_dimension=0, tiled=True)[0]
    sums = []
    offset = 0
    for w in widths:
        sums.append(mine[offset : offset + w])
        offset += w
    (g_gain_one, g_shift_one, g_querybias, g_valuebias, g_outbias,
     g_gain_two, g_shift_two, g_upbias, g_downbias) = sums

    return (
        encoded_back,
        grad_back,
        g_gain_one,
        g_shift_one,
        project_part,
        g_querybias,
        g_valuebias,
        output_part,
        g_outbias,
        g_gain_two,
        g_shift_two,
        up_part,
        g_upbias,
        down_part,
        g_downbias,
    )


def solution(mesh):
    n_dp, n_fsdp = mesh.shape["dp"], mesh.shape["fsdp"]
    rows = P(("dp", "fsdp"), None)
    matrix = P("dp", "fsdp")
    vector = P("dp")

    def step(*args):
        return local(n_dp, n_fsdp, *args)

    return jax.shard_map(
        step,
        mesh=mesh,
        in_specs=(rows, rows, rows, P(("dp", "fsdp")), vector, vector, matrix, vector, vector,
                  matrix, vector, vector, vector, matrix, vector, matrix, vector),
        out_specs=(rows, rows, vector, vector, matrix, vector, vector, matrix, vector, vector,
                   vector, matrix, vector, matrix, vector),
        check_vma=False,
    )
```

time: 722 us -> 720 us (level)
  local copies, waits for them, and re-layouts: 29.4 us -> 66.3 us
  blocking collectives: 160 us -> 126 us
  waiting for transfers between devices: 356 us -> 385 us
  matrix products: 94.3 us -> 75.5 us
    all_gather x4, waiting for transfers between devices: 42 us -> 106 us  [gather_matrix(): every = lax.all_gather(block, ('dp', 'fsdp'), axis=0, tiled=False)]
    reduce_scatter x5, waiting for transfers between devices: 299 us -> 258 us  [the longest x4 258 us: scatter_matrix(): lax.psum_scatter(grad.astype(jnp.bfloat16), 'dp', scatter_dimension=0, ti...]
    all_gather x4 -> x0, blocking collectives: 27.6 us -> none  [the longest x1 8.66 us: local(): lax.all_gather(project_weight, 'fsdp', axis=1, tiled=True)]
    reshape x0 -> x13, local copies, waits for them, and re-layouts: none -> 26.5 us  [the longest x4 25.9 us: gather_matrix(): every = every.reshape(n_dp, n_fsdp, rows, cols).transpose(0, 2, 1, 3)]
    dot_general x14, matrix products: 73.1 us -> 63 us  [matmul(): jnp.einsum(pattern, left_side, right_side, preferred_element_type=jnp.flo...]
    all_to_all x1, starting transfers between devices: 14.3 us -> 5.6 us  [local(): lax.all_to_all(cotangent, 'dp', split_axis=0, concat_axis=0, tiled=True)]
    dot_general x4, matrix products: 21.2 us -> 12.5 us  [the longest x1 6.88 us: local(): jnp.dot(activated, down_full, preferred_element_type=jnp.float32)]
    unnamed x108 -> x85, local copies, waits for them, and re-layouts: 18.6 us -> 27 us
  transfers between devices with their start and end apart: 16 -> 17, of which waited for: 5 -> 9; matrix products, arithmetic and copies ran while one was open for 17% -> 12% of each run, Pallas kernels for 0% -> 0%
where the time goes in v1:
time: 720 us; the launch traced here: 717 us
  waiting for transfers between devices  385 us (53%)
  blocking collectives  126 us (18%)
  matrix products  75.5 us (10%)
  local copies, waits for them, and re-layouts  66.3 us (9%)
  other arithmetic  25.1 us (3%)
  starting transfers between devices  22.8 us (3%)
  between operations  15.8 us (2%)
    reduce_scatter x4, waiting for transfers between devices, scatter_matrix(): lax.psum_scatter(grad.astype(jnp.bfloat16), 'dp', scatter_dimension=0, ti...  258 us
    unnamed x2, blocking collectives  126 us
    all_gather x4, waiting for transfers between devices, gather_matrix(): every = lax.all_gather(block, ('dp', 'fsdp'), axis=0, tiled=False)  106 us
    dot_general x14, matrix products, matmul(): jnp.einsum(pattern, left_side, right_side, preferred_element_type=jnp.flo...  63 us
    unnamed x85, local copies, waits for them, and re-layouts  27 us
    reshape x4, local copies, waits for them, and re-layouts, gather_matrix(): every = every.reshape(n_dp, n_fsdp, rows, cols).transpose(0, 2, 1, 3)  25.9 us
    all_to_all x1, waiting for transfers between devices, local(): lax.all_to_all(patches, 'dp', split_axis=0, concat_axis=0, tiled=True)  14.6 us
  transfers between devices with their start and end apart: 17, of which 9 were waited for; matrix products, arithmetic and copies ran while one was open for 12% of the time, Pallas kernels for 0%

profile of v1, /device:TPU:0, one launch (start us, length us, event | category | flops | bytes accessed | tf_op | source)
XLA Modules:
  0.0 716.6 jit_solution(4727964703437797031)
XLA Ops:
  9.5 7.4 %all-to-all-start = ((bf16[16,32,768]{2,1,0:T(8,128)(2,1)}), bf16[16,32,768]{2,1,0:T(8,128)(2,1)S(1)}, u32[]{:S(2)}, u32[]{:S(2)}) async-start(bf16[16,32,768]{2,1,0:T(8,128)(2,1)} %bitcast.168), calls=%async_computation | async-start | bytes 1572864 | tf_op jit(solution)/shard_map/all_to_all | solution.py:76
  21.6 14.6 %all-to-all-done = bf16[16,32,768]{2,1,0:T(8,128)(2,1)S(1)} async-done(((bf16[16,32,768]{2,1,0:T(8,128)(2,1)}), bf16[16,32,768]{2,1,0:T(8,128)(2,1)S(1)}, u32[]{:S(2)}, u32[]{:S(2)}) %all-to-all-start) | async-done | bytes 786464 | tf_op jit(solution)/shard_map/all_to_all | solution.py:76
  36.1 5.6 all-to-all-start.2
  43.6 68.6 %all-reduce = bf16[9216]{0:T(1024)(128)(2,1)S(1)} all-reduce(bf16[9216]{0:T(1024)(128)(2,1)S(1)} %dynamic-update-slice), channel_id=2, replica_groups=mesh['dp'=16,'fsdp'=2] {'dp'}, use_global_device_ids=true, to_apply=%add | all-reduce | flops 9216 | bytes 36864
  119.8 16.1 %all-gather.10.cloned.1.call-done = bf16[1536,1152]{1,0:T(8,128)(2,1)} async-done(((bf16[48,1152]{1,0:T(8,128)(2,1)}), bf16[1536,1152]{1,0:T(8,128)(2,1)}) %all-gather.10.cloned.1.call-update) | async-done | bytes 3538960 | tf_op jit(solution)/shard_map/all_gather | solution.py:43
  135.9 4.7 copy.68
  160.8 40.3 %all-gather.14.cloned.1.call-done = bf16[1536,1536]{1,0:T(8,128)(2,1)} async-done(((bf16[48,1536]{1,0:T(8,128)(2,1)}), bf16[1536,1536]{1,0:T(8,128)(2,1)}) %all-gather.14.cloned.1.call-update) | async-done | bytes 4718608 | tf_op jit(solution)/shard_map/all_gather | solution.py:43
  201.2 9.4 %copy.74 = bf16[16,2,48,1536]{3,1,2,0:T(2,128)(2,1)} copy(bf16[16,2,48,1536]{3,2,1,0:T(8,128)(2,1)} %bitcast.143) | data formatting | bytes 9437184 | tf_op jit(solution)/shard_map/reshape | solution.py:44
  210.5 5.7 copy.92
  216.3 49.5 %all-gather.16.cloned.1.call-done = bf16[6144,384]{1,0:T(8,128)(2,1)} async-done(((bf16[192,384]{1,0:T(8,128)(2,1)}), bf16[6144,384]{1,0:T(8,128)(2,1)}) %all-gather.16.cloned.1.call-update) | async-done | bytes 4718608 | tf_op jit(solution)/shard_map/all_gather | solution.py:43
  265.8 9.6 %copy.75 = bf16[16,2,192,384]{3,1,2,0:T(2,128)(2,1)} copy(bf16[16,2,192,384]{3,2,1,0:T(8,128)(2,1)} %bitcast.144) | data formatting | bytes 9437184 | tf_op jit(solution)/shard_map/reshape | solution.py:44
  281.9 6.7 convert_reduce_fusion
  292.6 4.9 convolution_convert_fusion.1
  301.5 4.5 convolution_convert_fusion.2
  313.2 9.0 %convert_reduce_fusion.4 = (f32[12,64]{1,0:T(8,128)S(1)}, bf16[12,64,512]{2,1,0:T(8,128)(2,1)}) fusion(bf16[512,12,64]{0,2,1:T(8,128)(2,1)} %bitcast.155, f32[12,512]{1,0:T(8,128)S(1)} %log_add_fusion, f32[12,512,512]{1,2,0:T(8,128)} %copy-done, pred[512,512]{0,1:T(8,128)(4,1)S(1)} %broadcast_compare_fusion), kind=kOutput, calls=%fused_computation.51 | convolution fusion | flops 416414976 | bytes 14445568 | tf_op jit(solution)/shard_map/hqk,qhe->khe/dot_general | solution.py:34
  322.2 9.6 %multiply_reduce_fusion = (f32[12,512]{1,0:T(8,128)S(1)}, f32[12,512,512]{1,2,0:T(8,128)}) fusion(f32[12,512]{1,0:T(8,128)S(1)} %log_add_fusion, f32[12,512,512]{1,2,0:T(8,128)} %copy-done, pred[512,512]{0,1:T(8,128)(4,1)S(1)} %broadcast_compare_fusion, bf16[512,12,64]{0,2,1:T(8,128)(2,1)S(1)} %bitcast.156, bf16[512,12,64]{0,2,1:T(8,128)(2,1)S(1)} %bitcast.154), kind=kOutput, calls=%fused_computation.2 | convolution fusion | flops 418375680 | bytes 27049984 | tf_op jit(solution)/shard_map/qhe,khe->hqk/dot_general | solution.py:34
  331.7 7.1 multiply_convert_fusion
  344.1 5.0 fusion.44
  357.8 6.9 multiply_convert_fusion.5
  368.7 39.1 %reduce-scatter.17.cloned.1.call-done = bf16[48,768]{1,0:T(8,128)(2,1)} async-done(((bf16[768,768]{1,0:T(8,128)(2,1)}), bf16[48,768]{1,0:T(8,128)(2,1)}) %reduce-scatter.17.cloned.1.call-update) | async-done | bytes 73744 | tf_op jit(solution)/shard_map/reduce_scatter | solution.py:49
  409.5 69.1 %reduce-scatter.15.cloned.1.call-done = bf16[48,2304]{1,0:T(8,128)(2,1)} async-done(((bf16[768,2304]{1,0:T(8,128)(2,1)}), bf16[48,2304]{1,0:T(8,128)(2,1)}) %reduce-scatter.15.cloned.1.call-update) | async-done | bytes 221200 | tf_op jit(solution)/shard_map/reduce_scatter | solution.py:49
  484.3 72.6 %reduce-scatter.23.cloned.1.call-done = bf16[192,768]{1,0:T(8,128)(2,1)} async-done(((bf16[3072,768]{1,0:T(8,128)(2,1)}), bf16[192,768]{1,0:T(8,128)(2,1)}) %reduce-scatter.23.cloned.1.call-update) | async-done | bytes 294928 | tf_op jit(solution)/shard_map/reduce_scatter | solution.py:49
  558.9 76.8 %reduce-scatter.19.cloned.1.call-done = bf16[48,3072]{1,0:T(8,128)(2,1)} async-done(((bf16[768,3072]{1,0:T(8,128)(2,1)}), bf16[48,3072]{1,0:T(8,128)(2,1)}) %reduce-scatter.19.cloned.1.call-update) | async-done | bytes 294928 | tf_op jit(solution)/shard_map/reduce_scatter | solution.py:49
  640.5 57.7 %all-reduce.1 = f32[16,576]{1,0:T(8,128)S(1)} all-reduce(f32[16,576]{1,0:T(8,128)S(1)} %add.163), channel_id=7, replica_groups=mesh['dp'=16,'fsdp'=2] {'dp'}, use_global_device_ids=true, to_apply=%region_23.24.clone | all-reduce | flops 9216 | bytes 73728
  (197 shorter events, 100.4 us)
Async XLA Ops:
  7.2 36.0 %copy-start.29 = (bf16[48]{0:T(256)(128)(2,1)S(1)}, bf16[48]{0:T(256)(128)(2,1)}, u32[]{:S(2)}) copy-start(bf16[48]{0:T(256)(128)(2,1)} %param.33) | copy-start | bytes 292
  7.2 36.0 %copy-start.28 = (bf16[192]{0:T(256)(128)(2,1)S(1)}, bf16[192]{0:T(256)(128)(2,1)}, u32[]{:S(2)}) copy-start(bf16[192]{0:T(256)(128)(2,1)} %param.31) | copy-start | bytes 1156
  7.2 36.0 %copy-start.27 = (bf16[48]{0:T(256)(128)(2,1)S(1)}, bf16[48]{0:T(256)(128)(2,1)}, u32[]{:S(2)}) copy-start(bf16[48]{0:T(256)(128)(2,1)} %param.29) | copy-start | bytes 292
  7.2 36.0 %copy-start.26 = (bf16[48]{0:T(256)(128)(2,1)S(1)}, bf16[48]{0:T(256)(128)(2,1)}, u32[]{:S(2)}) copy-start(bf16[48]{0:T(256)(128)(2,1)} %param.28) | copy-start | bytes 292
  7.2 36.0 %copy-start.25 = (bf16[48]{0:T(256)(128)(2,1)S(1)}, bf16[48]{0:T(256)(128)(2,1)}, u32[]{:S(2)}) copy-start(bf16[48]{0:T(256)(128)(2,1)} %param.27) | copy-start | bytes 292
  7.2 36.0 %copy-start.24 = (bf16[48]{0:T(256)(128)(2,1)S(1)}, bf16[48]{0:T(256)(128)(2,1)}, u32[]{:S(2)}) copy-start(bf16[48]{0:T(256)(128)(2,1)} %param.25) | copy-start | bytes 292
  7.3 109.1 %all-gather.12.cloned.1.call-start = ((), (), s32[]{:S(2)}) async-start(), calls=%async_computation.18 | async-start | bytes 1216512 | tf_op jit(solution)/shard_map/all_gather | solution.py:43
  8.0 127.9 %all-gather.10.cloned.1.call-start = ((), (), s32[]{:S(2)}) async-start(), calls=%async_computation.17 | async-start | bytes 3649536 | tf_op jit(solution)/shard_map/all_gather | solution.py:43
  8.8 192.4 %all-gather.14.cloned.1.call-start = ((), (), s32[]{:S(2)}) async-start(), calls=%async_computation.19 | async-start | bytes 4866048 | tf_op jit(solution)/shard_map/all_gather | solution.py:43
  9.5 26.6 %all-to-all-start = ((bf16[16,32,768]{2,1,0:T(8,128)(2,1)}), bf16[16,32,768]{2,1,0:T(8,128)(2,1)S(1)}, u32[]{:S(2)}, u32[]{:S(2)}) async-start(bf16[16,32,768]{2,1,0:T(8,128)(2,1)} %bitcast.168), calls=%async_computation | async-start | bytes 1572864 | tf_op jit(solution)/shard_map/all_to_all | solution.py:76
  16.9 248.9 %all-gather.16.cloned.1.call-start = ((), (), s32[]{:S(2)}) async-start(), calls=%async_computation.20 | async-start | bytes 4866048 | tf_op jit(solution)/shard_map/all_gather | solution.py:43
  36.1 77.8 %all-to-all-start.2 = ((bf16[16,32,768]{2,1,0:T(8,128)(2,1)}), bf16[16,32,768]{2,1,0:T(8,128)(2,1)S(1)}, u32[]{:S(2)}, u32[]{:S(2)}) async-start(bf16[16,32,768]{2,1,0:T(8,128)(2,1)} %bitcast.169), calls=%async_computation.2 | async-start | bytes 1572864 | tf_op jit(solution)/shard_map/all_to_all | solution.py:77
  41.8 366.0 %reduce-scatter.17.cloned.1.call-start = ((), (), s32[]{:S(2)}) async-start(), calls=%async_computation.13 | async-start | bytes 1253376 | tf_op jit(solution)/shard_map/reduce_scatter | solution.py:49
  160.5 137.0 %copy-start.5 = (f32[512,768]{1,0:T(8,128)}, f32[512,768]{1,0:T(8,128)S(1)}, u32[]{:S(2)}) copy-start(f32[512,768]{1,0:T(8,128)S(1)} %get-tuple-element.71) | copy-start | bytes 4718596
  343.8 134.8 %reduce-scatter.15.cloned.1.call-start = ((), (), s32[]{:S(2)}) async-start(), calls=%async_computation.12 | async-start | bytes 3760128 | tf_op jit(solution)/shard_map/reduce_scatter | solution.py:49
  355.6 201.4 %reduce-scatter.23.cloned.1.call-start = ((), (), s32[]{:S(2)}) async-start(), calls=%async_computation.16 | async-start | bytes 5013504 | tf_op jit(solution)/shard_map/reduce_scatter | solution.py:49
  356.4 279.3 %reduce-scatter.19.cloned.1.call-start = ((), (), s32[]{:S(2)}) async-start(), calls=%async_computation.14 | async-start | bytes 5013504 | tf_op jit(solution)/shard_map/reduce_scatter | solution.py:49
  364.7 116.0 %all-to-all-start.1 = ((bf16[16,32,768]{2,1,0:T(8,128)(2,1)}), bf16[16,32,768]{2,1,0:T(8,128)(2,1)S(1)}, u32[]{:S(2)}, u32[]{:S(2)}) async-start(bf16[16,32,768]{2,1,0:T(8,128)(2,1)} %bitcast.19), calls=%async_computation.1 | async-start | bytes 1572864 | tf_op jit(solution)/shard_map/all_to_all | solution.py:135
  368.6 332.2 %reduce-scatter.27.cloned.1.call-start = ((), (), s32[]{:S(2)}) async-start(), calls=%async_computation.22 | async-start | bytes 294912
  409.5 292.9 %reduce-scatter.25.cloned.1.call-start = ((), (), s32[]{:S(2)}) async-start(), calls=%async_computation.21 | async-start | bytes 884736
  480.6 220.1 %all-to-all-start.3 = ((bf16[16,32,768]{2,1,0:T(8,128)(2,1)}), bf16[16,32,768]{2,1,0:T(8,128)(2,1)S(1)}, u32[]{:S(2)}, u32[]{:S(2)}) async-start(bf16[16,32,768]{2,1,0:T(8,128)(2,1)} %bitcast.32), calls=%async_computation.3 | async-start | bytes 1572864 | tf_op jit(solution)/shard_map/all_to_all | solution.py:187
  484.3 220.0 %reduce-scatter.29.cloned.1.call-start = ((), (), s32[]{:S(2)}) async-start(), calls=%async_computation.23 | async-start | bytes 589824
  558.9 147.2 %reduce-scatter.21.cloned.1.call-start = ((), (), s32[]{:S(2)}) async-start(), calls=%async_computation.15 | async-start | bytes 442368 | tf_op jit(solution)/shard_map/reduce_scatter | solution.py:50
  636.5 4.1 collective-permute-start
  (28 other events, 265.1 us)
Sparse Core Ops, SparseCore 0:
  11.0 62.0 all-gather.11
  76.0 59.8 all-gather.9
  138.8 62.2 all-gather.13
  203.9 61.8 all-gather.15
  343.9 63.8 reduce-scatter.16
  411.5 67.0 reduce-scatter.14
  482.5 74.4 reduce-scatter.22
  560.8 74.8 reduce-scatter.18
  638.5 10.1 reduce-scatter.26
  651.4 15.3 reduce-scatter.24
  669.6 13.1 reduce-scatter.28
  684.9 12.0 reduce-scatter.20

commit v2 on v1

v2 whole, which is shorter than its diff:
```python
import math

import jax
import jax.numpy as jnp
import numpy as np
from jax import lax
from jax.sharding import Mesh
from jax.sharding import PartitionSpec as P

HEADS = 12
HEAD = 64


NORM_EPSILON = 1e-12
MASK_VALUE = -1e30
ROOT_HALF = 0.7071067811865476


def norm_rows(values, norm_gain, norm_shift):
    center = values - jnp.mean(values, axis=-1, keepdims=True)
    spread = jnp.mean(center * center, axis=-1, keepdims=True)
    return center * lax.rsqrt(spread + NORM_EPSILON) * norm_gain + norm_shift


def gelu_exact(values):
    return 0.5 * values * (1.0 + lax.erf(values * ROOT_HALF))


def slot_labels(lengths, arrange):
    total_rows = arrange.shape[0]
    slot_ends = jnp.cumsum(lengths[0])
    position = jnp.arange(total_rows, dtype=jnp.int32)
    slot_index = jnp.sum((position[:, None] >= slot_ends[None, :]).astype(jnp.int32), axis=1)
    return jnp.zeros((total_rows,), jnp.int32).at[arrange].set(slot_index)


def matmul(left_side, right_side, pattern):
    return jnp.einsum(pattern, left_side, right_side, preferred_element_type=jnp.float32)


def column_sums(values):
    return jnp.sum(values.astype(jnp.float32), axis=0)


def physical_axes(mesh):
    line = mesh.devices[:, 0]
    n = len(line)

    def key(d):
        return (*d.coords, d.core_on_chip)

    try:
        first = key(line[0])
        found = []
        for ci in range(len(first)):
            values = {key(d)[ci] for d in line}
            if len(values) > 1:
                change = min(i for i in range(n) if key(line[i])[ci] != first[ci])
                found.append((change, len(values), ci))
        found.sort()
        stride = 1
        for change, size, _ in found:
            assert change == stride
            stride *= size
        assert stride == n
        sizes = [size for _, size, _ in found][::-1]
        core_at = [ci for _, _, ci in found][::-1].index(len(first) - 1)
    except (AssertionError, AttributeError, TypeError, ValueError):
        sizes, core_at = [n], None
    return sizes, core_at


class Tree:
    def __init__(self, canon, first, others, last):
        self.canon = canon
        self.first = first
        self.others = others
        self.last = last
        self.half = first[1] // 2 if first[1] % 2 == 0 else first[1]
        orders = [others, others[::-1]] if self.half < first[1] else [others]
        self.parts = []
        for order in orders:
            stages = list(order) + ([last] if last else [])
            self.parts.append(stages)

    def count(self):
        return math.prod(k for _, k in self.canon)

    def _part_axes(self, stages, size_first):
        return [ax for ax in stages[::-1]] + [(self.first[0], size_first)]

    def _index_tables(self):
        me = {name: lax.axis_index(name) for name, _ in self.canon}
        sizes = [k for _, k in self.canon]
        grids = jnp.meshgrid(*[jnp.arange(k, dtype=jnp.int32) for k in sizes], indexing="ij")
        actual = {name: g for (name, _), g in zip(self.canon, grids)}
        rel = {name: (me[name] - actual[name]) % k for name, k in self.canon}
        f_name = self.first[0]
        flat = jnp.zeros(sizes, jnp.int32)
        offset = 0
        pieces = []
        for p, stages in enumerate(self.parts):
            size_first = self.half if len(self.parts) > 1 else self.first[1]
            axes = self._part_axes(stages, size_first)
            index = jnp.zeros(sizes, jnp.int32)
            for name, k in axes:
                r = rel[name]
                if name == f_name:
                    r = r - p * self.half
                index = index * k + r
            pieces.append((offset, index))
            offset += math.prod(k for _, k in axes)
        if len(pieces) == 1:
            flat = pieces[0][1]
        else:
            in_first = rel[f_name] < self.half
            flat = jnp.where(in_first, pieces[0][1], pieces[1][0] + pieces[1][1])
        return flat.reshape(-1)

    def gather(self, block):
        f_name, f_k = self.first
        cur = _stage_gather(block, f_name, f_k)
        parts = []
        for p, stages in enumerate(self.parts):
            piece = cur[p * self.half : (p + 1) * self.half] if len(self.parts) > 1 else cur
            for name, k in stages:
                piece = _stage_gather(piece, name, k)
            parts.append(piece.reshape(-1, *block.shape))
        joined = jnp.concatenate(parts) if len(parts) > 1 else parts[0]
        return jnp.take(joined, self._index_tables(), axis=0)

    def scatter(self, blocks, send_dtype):
        table = self._index_tables()
        inverse = jnp.zeros_like(table).at[table].set(jnp.arange(table.shape[0], dtype=jnp.int32))
        relative = jnp.take(blocks, inverse, axis=0)
        shape = blocks.shape[1:]
        f_name, f_k = self.first
        ends = []
        offset = 0
        for p, stages in enumerate(self.parts):
            size_first = self.half if len(self.parts) > 1 else f_k
            axes = self._part_axes(stages, size_first)
            n = math.prod(k for _, k in axes)
            piece = relative[offset : offset + n].reshape(*[k for _, k in axes], *shape)
            offset += n
            for name, k in stages[::-1]:
                piece = _stage_scatter(piece, name, k, send_dtype)
            ends.append(piece)
        joined = jnp.concatenate(ends) if len(ends) > 1 else ends[0]
        return _stage_scatter(joined, f_name, f_k, send_dtype)


def _stage_gather(cur, name, k):
    outs = [cur] + [lax.ppermute(cur, name, [(i, (i + s) % k) for i in range(k)]) for s in range(1, k)]
    return jnp.stack(outs)


def _stage_scatter(cur, name, k, send_dtype):
    total = cur[0].astype(jnp.float32)
    for s in range(1, k):
        got = lax.ppermute(cur[s].astype(send_dtype), name, [(i, (i - s) % k) for i in range(k)])
        total = total + got.astype(jnp.float32)
    return total


def build(mesh):
    n_dp, n_fsdp = mesh.shape["dp"], mesh.shape["fsdp"]
    sizes, core_at = physical_axes(mesh)
    names = [f"d{i}" for i in range(len(sizes))]
    phys = Mesh(mesh.devices.reshape(*sizes, n_fsdp), (*names, "fsdp"))
    dp_axes = list(zip(names, sizes))
    last = dp_axes[core_at] if core_at is not None and len(dp_axes) > 1 else None
    external = [ax for ax in dp_axes if ax != last]
    first = max(external, key=lambda ax: ax[1])
    rest = [ax for ax in external if ax != first]
    weights = Tree([("fsdp", n_fsdp)] + dp_axes, first, rest + [("fsdp", n_fsdp)], last)
    vectors = Tree(dp_axes, first, rest, last)
    return phys, tuple(names), weights, vectors


def local(dp_names, weights_tree, vectors_tree, n_dp, n_fsdp, patches, cotangent, lengths, arrange,
          first_gain, first_shift, project_weight, query_bias, value_bias, output_weight, output_bias,
          second_gain, second_shift, up_weight, up_bias, down_weight, down_bias):
    arrived = lax.all_to_all(patches, dp_names, split_axis=0, concat_axis=0, tiled=True)
    cot_rows = lax.all_to_all(cotangent, dp_names, split_axis=0, concat_axis=0, tiled=True)
    total_rows, width = patches.shape
    labels = slot_labels(lengths, arrange)
    live_rows = (labels < lengths.shape[1]).astype(jnp.float32)[:, None]

    vector_parts = (
        first_gain, first_shift, query_bias, value_bias, output_bias,
        second_gain, second_shift, up_bias, down_bias,
    )
    widths = [v.shape[0] for v in vector_parts]
    packed = vectors_tree.gather(jnp.concatenate(vector_parts))
    vectors = []
    offset = 0
    for w in widths:
        vectors.append(packed[:, offset : offset + w].reshape(-1).astype(jnp.float32))
        offset += w
    gain_one, shift_one, query_full, value_full, outbias_full, gain_two, shift_two, upbias_full, downbias_full = vectors

    def gather_matrix(block):
        rows, cols = block.shape
        every = weights_tree.gather(block)
        return every.reshape(n_fsdp, n_dp * rows, cols)

    project_full = gather_matrix(project_weight)
    output_full = gather_matrix(output_weight)
    up_full = gather_matrix(up_weight)
    down_full = gather_matrix(down_weight)

    def split_cols(values):
        return values.reshape(values.shape[0], n_fsdp, -1)

    def forward_dot(left, matrix):
        out = matmul(left, matrix, "td,jdc->tjc")
        return out.reshape(out.shape[0], -1)

    def backward_dot(grad, matrix):
        return matmul(split_cols(grad), matrix, "tjc,jdc->td")

    def weight_grad(left, grad):
        out = matmul(left, split_cols(grad), "td,tjc->jdc")
        return out.astype(jnp.bfloat16)

    def scatter_matrix(grad_low, rows):
        blocks = grad_low.reshape(n_fsdp * n_dp, rows, grad_low.shape[-1])
        return weights_tree.scatter(blocks, jnp.bfloat16)

    inputs = arrived.astype(jnp.float32)
    normed_one = norm_rows(inputs, gain_one, shift_one)
    normed_low = normed_one.astype(jnp.bfloat16)
    joint = forward_dot(normed_low, project_full)
    queries = (joint[:, :width] + query_full).astype(jnp.bfloat16).reshape(total_rows, HEADS, HEAD)
    key_rows = joint[:, width : 2 * width].astype(jnp.bfloat16).reshape(total_rows, HEADS, HEAD)
    value_rows = (joint[:, 2 * width :] + value_full).astype(jnp.bfloat16).reshape(total_rows, HEADS, HEAD)
    score_scale = HEAD ** (-0.5)
    visible = labels[:, None] == labels[None, :]

    def block_scores():
        raw_scores = matmul(queries, key_rows, "qhe,khe->hqk") * score_scale
        return jnp.where(visible[None], raw_scores, MASK_VALUE)

    scores = block_scores()
    top_score = jnp.max(scores, axis=-1, keepdims=True)
    weights = jnp.exp(scores - top_score)
    totals = jnp.sum(weights, axis=-1, keepdims=True)
    prob_low = (weights / totals).astype(jnp.bfloat16)
    mixed_rows = matmul(prob_low, value_rows, "hqk,khe->qhe")
    log_totals = top_score + jnp.log(totals)
    attended = mixed_rows.astype(jnp.bfloat16).reshape(total_rows, width)
    attn_out = forward_dot(attended, output_full) + outbias_full
    hidden = inputs + attn_out
    normed_two = norm_rows(hidden, gain_two, shift_two)
    normed_two_low = normed_two.astype(jnp.bfloat16)
    pre_act = forward_dot(normed_two_low, up_full) + upbias_full
    activated = gelu_exact(pre_act).astype(jnp.bfloat16)
    branch = forward_dot(activated, down_full) + downbias_full
    encoded_rows = live_rows * (hidden + branch)
    encoded_back = lax.all_to_all(
        encoded_rows.astype(jnp.bfloat16), dp_names, split_axis=0, concat_axis=0, tiled=True
    )

    grad_out = live_rows * cot_rows.astype(jnp.float32)
    grad_branch = grad_out.astype(jnp.bfloat16)
    down_low = weight_grad(activated, grad_branch)
    grad_downbias = column_sums(grad_branch)
    grad_activ = backward_dot(grad_branch, down_full)
    grad_pre = jax.vjp(gelu_exact, pre_act)[1](grad_activ)[0].astype(jnp.bfloat16)
    up_low = weight_grad(normed_two_low, grad_pre)
    grad_upbias = column_sums(grad_pre)
    grad_normed_two = backward_dot(grad_pre, up_full)
    norm_pull_two = jax.vjp(norm_rows, hidden, gain_two, shift_two)[1]
    grad_hidden_part, grad_gain_two, grad_shift_two = norm_pull_two(grad_normed_two)
    grad_hidden = grad_out + grad_hidden_part
    grad_hidden, down_low, up_low = lax.optimization_barrier((grad_hidden, down_low, up_low))
    down_part = scatter_matrix(down_low, down_weight.shape[0])
    up_part = scatter_matrix(up_low, up_weight.shape[0])

    grad_attn = grad_hidden.astype(jnp.bfloat16)
    output_low = weight_grad(attended, grad_attn)
    grad_outbias = column_sums(grad_attn)
    grad_attended = backward_dot(grad_attn, output_full).astype(jnp.bfloat16).reshape(total_rows, HEADS, HEAD)
    grad_attended, output_low = lax.optimization_barrier((grad_attended, output_low))
    output_part = scatter_matrix(output_low, output_weight.shape[0])

    scores = block_scores()
    prob_full = jnp.exp(scores - log_totals)
    prob_low = prob_full.astype(jnp.bfloat16)
    value_grad = matmul(prob_low, grad_attended, "hqk,qhe->khe")
    grad_prob = matmul(grad_attended, value_rows, "qhe,khe->hqk")
    inner = jnp.sum(prob_full * grad_prob, axis=-1, keepdims=True)
    grad_scores = (prob_full * (grad_prob - inner)).astype(jnp.bfloat16)
    query_grad = matmul(grad_scores, key_rows, "hqk,khe->qhe") * score_scale
    key_grad = matmul(grad_scores, queries, "hqk,qhe->khe") * score_scale
    grad_queries = query_grad.astype(jnp.bfloat16).reshape(total_rows, width)
    grad_keys = key_grad.reshape(total_rows, width).astype(jnp.bfloat16)
    grad_values = value_grad.reshape(total_rows, width).astype(jnp.bfloat16)
    grad_joint = jnp.concatenate([grad_queries, grad_keys, grad_values], axis=1)
    project_low = weight_grad(normed_low, grad_joint)
    grad_querybias = column_sums(grad_queries)
    grad_valuebias = column_sums(grad_values)
    project_part = scatter_matrix(project_low, project_weight.shape[0])
    grad_normed_one = backward_dot(grad_joint, project_full)
    norm_pull_one = jax.vjp(norm_rows, inputs, gain_one, shift_one)[1]
    grad_input_part, grad_gain_one, grad_shift_one = norm_pull_one(grad_normed_one)
    grad_inputs = grad_hidden + grad_input_part
    grad_back = lax.all_to_all(
        grad_inputs.astype(jnp.bfloat16), dp_names, split_axis=0, concat_axis=0, tiled=True
    )

    vector_grads = (
        grad_gain_one, grad_shift_one, grad_querybias, grad_valuebias, grad_outbias,
        grad_gain_two, grad_shift_two, grad_upbias, grad_downbias,
    )
    stacked = jnp.concatenate([g.reshape(n_dp, -1) for g in vector_grads], axis=1)
    stacked = stacked + lax.ppermute(stacked, "fsdp", [(i, (i + 1) % n_fsdp) for i in range(n_fsdp)])
    mine = vectors_tree.scatter(stacked, jnp.float32)
    sums = []
    offset = 0
    for w in widths:
        sums.append(mine[offset : offset + w])
        offset += w
    (g_gain_one, g_shift_one, g_querybias, g_valuebias, g_outbias,
     g_gain_two, g_shift_two, g_upbias, g_downbias) = sums

    return (
        encoded_back, grad_back, g_gain_one, g_shift_one, project_part, g_querybias, g_valuebias,
        output_part, g_outbias, g_gain_two, g_shift_two, up_part, g_upbias, down_part, g_downbias,
    )


def solution(mesh):
    n_dp, n_fsdp = mesh.shape["dp"], mesh.shape["fsdp"]
    phys, dp_names, weights_tree, vectors_tree = build(mesh)
    rows = P((*dp_names, "fsdp"), None)
    matrix = P(dp_names, "fsdp")
    vector = P(dp_names)

    def step(*args):
        return local(dp_names, weights_tree, vectors_tree, n_dp, n_fsdp, *args)

    return jax.shard_map(
        step,
        mesh=phys,
        in_specs=(rows, rows, rows, P((*dp_names, "fsdp")), vector, vector, matrix, vector, vector,
                  matrix, vector, vector, vector, matrix, vector, matrix, vector),
        out_specs=(rows, rows, vector, vector, matrix, vector, vector, matrix, vector, vector,
                   vector, matrix, vector, matrix, vector),
        check_vma=False,
    )
```

time: 720 us -> 560 us (0.78)
  waiting for transfers between devices: 385 us -> 115 us
  blocking collectives: 126 us -> 0 us
  starting transfers between devices: 22.8 us -> 115 us
  local copies, waits for them, and re-layouts: 66.3 us -> 146 us
  other arithmetic: 25.1 us -> 98.2 us
  between operations: 15.8 us -> 2.53 us
    reduce_scatter x5 -> x0, waiting for transfers between devices: 258 us -> none  [the longest x4 258 us: scatter_matrix(): lax.psum_scatter(grad.astype(jnp.bfloat16), 'dp', scatter_dimension=0, ti...]
    unnamed x2 -> x0, blocking collectives: 126 us -> none
    ppermute x0 -> x86, waiting for transfers between devices: none -> 107 us  [the longest x43 68.7 us: _stage_scatter(): lax.ppermute(cur[s].astype(send_dtype), name, [(i, (i - s) % k) for i in...]
    all_gather x4 -> x0, waiting for transfers between devices: 106 us -> none  [gather_matrix(): every = lax.all_gather(block, ('dp', 'fsdp'), axis=0, tiled=False)]
    ppermute x0 -> x86, starting transfers between devices: none -> 93.3 us  [the longest x43 49.4 us: _stage_gather(): lax.ppermute(cur, name, [(i, (i + s) % k) for i in range(k)])]
    gather x0 -> x10, local copies, waits for them, and re-layouts: none -> 36.7 us  [the longest x5 19.6 us: scatter(): relative = jnp.take(blocks, inverse, axis=0)]
    dot_general x0 -> x4, local copies, waits for them, and re-layouts: none -> 32.9 us  [matmul(): jnp.einsum(pattern, left_side, right_side, preferred_element_type=jnp.flo...]
    another operation x1 -> x47, other arithmetic: 0.83 us -> 33 us  [the longest x42 32 us: _stage_gather(): return jnp.stack(outs)]
  transfers between devices with their start and end apart: 17 -> 91, of which waited for: 9 -> 33; matrix products, arithmetic and copies ran while one was open for 12% -> 36% of each run, Pallas kernels for 0% -> 0%
where the time goes in v2:
time: 560 us; the launch traced here: 556 us
  local copies, waits for them, and re-layouts  146 us (26%)
  starting transfers between devices  115 us (21%)
  waiting for transfers between devices  115 us (21%)
  other arithmetic  98.2 us (18%)
  matrix products  79.7 us (14%)
    dot_general x18, matrix products, matmul(): jnp.einsum(pattern, left_side, right_side, preferred_element_type=jnp.flo...  79.7 us
    ppermute x43, waiting for transfers between devices, _stage_scatter(): lax.ppermute(cur[s].astype(send_dtype), name, [(i, (i - s) % k) for i in...  68.7 us
    ppermute x43, starting transfers between devices, _stage_gather(): lax.ppermute(cur, name, [(i, (i + s) % k) for i in range(k)])  49.4 us
    ppermute x43, starting transfers between devices, _stage_scatter(): lax.ppermute(cur[s].astype(send_dtype), name, [(i, (i - s) % k) for i in...  43.9 us
    ppermute x43, waiting for transfers between devices, _stage_gather(): lax.ppermute(cur, name, [(i, (i + s) % k) for i in range(k)])  38 us
    dot_general x4, local copies, waits for them, and re-layouts, matmul(): jnp.einsum(pattern, left_side, right_side, preferred_element_type=jnp.flo...  32.9 us
    another operation x42, other arithmetic, _stage_gather(): return jnp.stack(outs)  32 us
    gather x5, local copies, waits for them, and re-layouts, scatter(): relative = jnp.take(blocks, inverse, axis=0)  19.6 us
  transfers between devices with their start and end apart: 91, of which 33 were waited for; matrix products, arithmetic and copies ran while one was open for 36% of the time, Pallas kernels for 0%

profile of v2, /device:TPU:0, one launch (start us, length us, event | category | flops | bytes accessed | tf_op | source)
XLA Modules:
  0.0 556.2 jit_solution(18325906292859050898)
XLA Ops:
  0.7 6.1 %concatenate.34 = bf16[576]{0:T(1024)(128)(2,1)S(1)} concatenate(bf16[48]{0:T(256)(128)(2,1)} %param.29, bf16[48]{0:T(256)(128)(2,1)} %param.30, bf16[48]{0:T(256)(128)(2,1)} %param.32, bf16[48]{0:T(256)(128)(2,1)} %param.33, bf16[48]{0:T(256)(128)(2,1)} %param.35, bf16[48]{0:T(256)(128)(2,1)} %param.36, bf16[48]{0:T(256)(128)(2,1)} %param.37, bf16[192]{0:T(256)(128)(2,1)} %param.39, ...), dimensions={0} | concatenate | bytes 2304 | tf_op jit(solution)/shard_map/concatenate | solution.py:195
  14.9 5.7 %all-to-all-start = ((bf16[16,32,768]{2,1,0:T(8,128)(2,1)}), bf16[16,32,768]{2,1,0:T(8,128)(2,1)S(1)}, u32[]{:S(2)}, u32[]{:S(2)}) async-start(bf16[16,32,768]{2,1,0:T(8,128)(2,1)} %bitcast.528), calls=%async_computation | async-start | bytes 1572864 | tf_op jit(solution)/shard_map/all_to_all | solution.py:184
  109.0 5.8 %all-to-all-start.2 = ((bf16[16,32,768]{2,1,0:T(8,128)(2,1)}), bf16[16,32,768]{2,1,0:T(8,128)(2,1)S(1)}, u32[]{:S(2)}, u32[]{:S(2)}) async-start(bf16[16,32,768]{2,1,0:T(8,128)(2,1)} %bitcast.529), calls=%async_computation.2 | async-start | bytes 1572864 | tf_op jit(solution)/shard_map/all_to_all | solution.py:185
  123.6 13.2 %collective-permute-done.41 = bf16[2,2,192,384]{3,2,1,0:T(8,128)(2,1)} collective-permute-done((bf16[2,2,192,384]{3,2,1,0:T(8,128)(2,1)}, bf16[2,2,192,384]{3,2,1,0:T(8,128)(2,1)}, u32[]{:S(2)}, u32[]{:S(2)}) %collective-permute-start.41) | collective-permute-done | bytes 589856 | tf_op jit(solution)/shard_map/ppermute | solution.py:154
  162.6 5.9 %copy.127 = bf16[2,1152,768]{2,1,0:T(8,128)(2,1)} copy(bf16[2,1152,768]{1,2,0:T(8,128)(2,1)} %bitcast.481) | data formatting | bytes 7077888 | tf_op jit(solution)/shard_map/td,jdc->tjc/dot_general | solution.py:38
  207.0 18.9 %copy.133 = bf16[2,1536,768]{2,1,0:T(8,128)(2,1)} copy(bf16[2,1536,768]{1,2,0:T(8,128)(2,1)} %bitcast.475) | data formatting | bytes 9437184 | tf_op jit(solution)/shard_map/td,jdc->tjc/dot_general | solution.py:38
  232.1 5.6 %gather_fusion.5 = bf16[32,192,384]{2,1,0:T(8,128)(2,1)} fusion(bf16[32,192,384]{2,1,0:T(8,128)(2,1)} %pad_maximum_fusion.1, s32[1024]{0:T(1024)S(1)} %pad_clamp_fusion.2), kind=kCustom, calls=%fused_computation.3.clone | custom fusion | bytes 9437312 | tf_op jit(solution)/shard_map/jit(_take)/gather | solution.py:130
  240.7 8.0 %multiply_convert_fusion.1 = (bf16[512,3072]{1,0:T(8,128)(2,1)}, f32[512,3072]{1,0:T(8,128)S(1)}) fusion(f32[3072]{0:T(1024)S(1)} %reshape.1088, bf16[3072,768]{1,0:T(8,128)(2,1)} %bitcast.502, f32[512,768]{1,0:T(8,128)S(1)} %get-tuple-element.147, f32[768]{0:T(1024)S(1)} %reshape.1087, f32[768]{0:T(1024)S(1)} %reshape.1086, f32[512]{0:T(512)S(1)} %fusion.91, ...), kind=kOutput, calls=%fused_computation.32 | convolution fusion | flops 2427322368 | bytes 15751168 | tf_op jit(solution)/shard_map/td,jdc->tjc/dot_general | solution.py:38
  248.7 8.5 %convert_reduce_fusion = (f32[3072]{0:T(1024)S(1)}, bf16[512,3072]{1,0:T(8,128)(2,1)}) fusion(bf16[2,3072,384]{2,1,0:T(8,128)(2,1)S(1)} %bitcast.473, f32[512,2,384]{2,1,0:T(2,128)S(1)} %copy-done.41, f32[512]{0:T(512)S(1)} %compare_convert_fusion, f32[512,3072]{1,0:T(8,128)S(1)} %get-tuple-element.149, f32[3072]{0:T(1024)S(1)} %reshape.1088), kind=kOutput, calls=%fused_computation.30 | convolution fusion | flops 2441868288 | bytes 15755264 | tf_op jit(solution)/shard_map/tjc,jdc->td/dot_general | solution.py:38
  262.0 7.4 %convert_bitcast_fusion = bf16[2,768,1536]{1,2,0:T(8,128)(2,1)} fusion(bf16[512,2,1536]{0,2,1:T(8,128)(2,1)} %bitcast.511, f32[512,768]{1,0:T(8,128)} %copy-done.12, f32[768]{0:T(1024)S(1)} %reshape.1087, f32[768]{0:T(1024)S(1)} %reshape.1086, f32[512]{0:T(512)S(1)} %fusion.91, f32[512]{0:T(512)S(1)} %broadcast_multiply_fusion.1), kind=kOutput, calls=%fused_computation.38 | convolution fusion | flops 2420244480 | bytes 9447424 | tf_op jit(solution)/shard_map/td,tjc->jdc/dot_general | solution.py:38
  288.5 11.4 %multiply_reduce_fusion = (f32[12,512]{1,0:T(8,128)S(1)}, f32[12,512,512]{1,2,0:T(8,128)}) fusion(f32[12,512]{1,0:T(8,128)S(1)} %log_add_fusion, f32[12,512,512]{1,2,0:T(8,128)} %copy-done, pred[512,512]{0,1:T(8,128)(4,1)S(1)} %broadcast_compare_fusion, bf16[512,12,64]{0,2,1:T(8,128)(2,1)} %bitcast.509, bf16[512,12,64]{0,2,1:T(8,128)(2,1)S(1)} %bitcast.508), kind=kOutput, calls=%fused_computation.14 | convolution fusion | flops 418375680 | bytes 27049984 | tf_op jit(solution)/shard_map/qhe,khe->hqk/dot_general | solution.py:38
  301.3 7.4 %multiply_convert_fusion = bf16[12,512,512]{1,2,0:T(8,128)(2,1)S(1)} fusion(f32[12,512,512]{1,2,0:T(8,128)} %get-tuple-element.152, f32[12,512]{1,0:T(8,128)S(1)} %get-tuple-element.151, f32[12,512]{1,0:T(8,128)S(1)} %log_add_fusion, f32[12,512,512]{1,2,0:T(8,128)S(1)} %bitcast.472, pred[512,512]{0,1:T(8,128)(4,1)S(1)} %broadcast_compare_fusion), kind=kLoop, calls=%fused_computation.13 | loop fusion | flops 18874368 | bytes 31768576 | tf_op jit(solution)/shard_map/convert_element_type | solution.py:294
  316.8 6.6 %copy.151 = bf16[2,3072,384]{2,1,0:T(8,128)(2,1)} copy(bf16[2,3072,384]{1,2,0:T(8,128)(2,1)} %fusion.12) | data formatting | bytes 9437184 | tf_op jit(solution)/shard_map/optimization_barrier | solution.py:277
  323.4 5.8 %gather_fusion.9 = bf16[32,192,384]{2,1,0:T(8,128)(2,1)} fusion(bf16[32,192,384]{2,1,0:T(8,128)(2,1)} %bitcast.479, s32[1024]{0:T(1024)S(1)} %pad_clamp_fusion), kind=kCustom, calls=%fused_computation.7.clone | custom fusion | bytes 9437312 | tf_op jit(solution)/shard_map/jit(_take)/gather | solution.py:135
  335.1 6.6 %copy.150 = bf16[2,768,1536]{2,1,0:T(8,128)(2,1)} copy(bf16[2,768,1536]{1,2,0:T(8,128)(2,1)} %convert_bitcast_fusion) | data formatting | bytes 9437184 | tf_op jit(solution)/shard_map/optimization_barrier | solution.py:277
  383.2 5.5 all-to-all-start.3
  388.8 6.7 %copy.134 = bf16[2,384,3072]{2,1,0:T(8,128)(2,1)} copy(bf16[2,384,3072]{1,2,0:T(8,128)(2,1)} %bitcast.474) | data formatting | bytes 9437184 | tf_op jit(solution)/shard_map/td,jdc->tjc/dot_general | solution.py:38
  396.8 6.8 %multiply_convert_fusion.5 = bf16[512,768]{1,0:T(8,128)(2,1)} fusion(f32[512,768]{1,0:T(8,128)S(1)} %copy-done.14, bf16[512,3072]{1,0:T(8,128)(2,1)} %get-tuple-element.148, bf16[768,3072]{1,0:T(8,128)(2,1)} %bitcast.501, f32[768]{0:T(1024)S(1)} %copy-done.64, f32[512]{0:T(512)S(1)} %compare_convert_fusion), kind=kOutput, calls=%fused_computation.106 | convolution fusion | flops 2417491968 | bytes 10228736 | tf_op jit(solution)/shard_map/td,jdc->tjc/dot_general | solution.py:38
  458.9 13.9 %collective-permute-done.57 = bf16[2,48,1152]{2,1,0:T(8,128)(2,1)S(1)} collective-permute-done((bf16[2,48,1152]{2,1,0:T(8,128)(2,1)S(1)}, bf16[2,48,1152]{2,1,0:T(8,128)(2,1)S(1)}, u32[]{:S(2)}, u32[]{:S(2)}) %collective-permute-start.57) | collective-permute-done | bytes 221216 | tf_op jit(solution)/shard_map/ppermute | solution.py:161
  487.2 8.6 %all-to-all-done.1 = bf16[16,32,768]{2,1,0:T(8,128)(2,1)S(1)} async-done(((bf16[16,32,768]{2,1,0:T(8,128)(2,1)}), bf16[16,32,768]{2,1,0:T(8,128)(2,1)S(1)}, u32[]{:S(2)}, u32[]{:S(2)}) %all-to-all-start.1) | async-done | bytes 786464 | tf_op jit(solution)/shard_map/all_to_all | solution.py:261
  495.7 9.3 %collective-permute-done.58 = bf16[48,1152]{1,0:T(8,128)(2,1)S(1)} collective-permute-done((bf16[48,1152]{1,0:T(8,128)(2,1)}, bf16[48,1152]{1,0:T(8,128)(2,1)S(1)}, u32[]{:S(2)}, u32[]{:S(2)}) %collective-permute-start.58) | collective-permute-done | bytes 110624 | tf_op jit(solution)/shard_map/ppermute | solution.py:161
  513.8 7.7 %collective-permute-done.74 = bf16[2,2,48,1536]{3,2,1,0:T(8,128)(2,1)S(1)} collective-permute-done((bf16[2,2,48,1536]{3,2,1,0:T(8,128)(2,1)}, bf16[2,2,48,1536]{3,2,1,0:T(8,128)(2,1)S(1)}, u32[]{:S(2)}, u32[]{:S(2)}) %collective-permute-start.74) | collective-permute-done | bytes 589856 | tf_op jit(solution)/shard_map/ppermute | solution.py:161
  535.6 8.1 %collective-permute-done.85 = bf16[192,384]{1,0:T(8,128)(2,1)S(1)} collective-permute-done((bf16[192,384]{1,0:T(8,128)(2,1)S(1)}, bf16[192,384]{1,0:T(8,128)(2,1)S(1)}, u32[]{:S(2)}, u32[]{:S(2)}) %collective-permute-start.85) | collective-permute-done | bytes 147488 | tf_op jit(solution)/shard_map/ppermute | solution.py:161
  545.2 7.0 %collective-permute-done.76 = bf16[48,1536]{1,0:T(8,128)(2,1)S(1)} collective-permute-done((bf16[48,1536]{1,0:T(8,128)(2,1)S(1)}, bf16[48,1536]{1,0:T(8,128)(2,1)S(1)}, u32[]{:S(2)}, u32[]{:S(2)}) %collective-permute-start.76) | collective-permute-done | bytes 147488 | tf_op jit(solution)/shard_map/ppermute | solution.py:161
  (582 shorter events, 357.0 us)
Async XLA Ops:
  9.9 23.6 %collective-permute-start.3 = (bf16[576]{0:T(1024)(128)(2,1)S(1)}, bf16[576]{0:T(1024)(128)(2,1)S(1)}, u32[]{:S(2)}, u32[]{:S(2)}) collective-permute-start(bf16[576]{0:T(1024)(128)(2,1)S(1)} %concatenate.34), channel_id=1, source_target_pairs={{0,16},{8,24},{16,0},{24,8},{1,17},{9,25},{17,1},{25,9},{2,18},{10... | collective-permute-start | bytes 3464 | tf_op jit(solution)/shard_map/ppermute | solution.py:154
  13.9 41.0 %collective-permute-start.7 = (bf16[48,1152]{1,0:T(8,128)(2,1)}, bf16[48,1152]{1,0:T(8,128)(2,1)S(1)}, u32[]{:S(2)}, u32[]{:S(2)}) collective-permute-start(bf16[48,1152]{1,0:T(8,128)(2,1)} %param.31), channel_id=1, source_target_pairs={{0,8},{8,16},{16,24},{24,0},{1,9},{9,17},{17,25},{25,1},{2,10},{10... | collective-permute-start | bytes 331784 | tf_op jit(solution)/shard_map/ppermute | solution.py:154
  14.6 40.5 %collective-permute-start.11 = (bf16[48,1152]{1,0:T(8,128)(2,1)}, bf16[48,1152]{1,0:T(8,128)(2,1)S(1)}, u32[]{:S(2)}, u32[]{:S(2)}) collective-permute-start(bf16[48,1152]{1,0:T(8,128)(2,1)} %param.31), channel_id=1, source_target_pairs={{0,16},{8,24},{16,0},{24,8},{1,17},{9,25},{17,1},{25,9},{2,18},{10... | collective-permute-start | bytes 331784 | tf_op jit(solution)/shard_map/ppermute | solution.py:154
  14.9 94.1 %all-to-all-start = ((bf16[16,32,768]{2,1,0:T(8,128)(2,1)}), bf16[16,32,768]{2,1,0:T(8,128)(2,1)S(1)}, u32[]{:S(2)}, u32[]{:S(2)}) async-start(bf16[16,32,768]{2,1,0:T(8,128)(2,1)} %bitcast.528), calls=%async_computation | async-start | bytes 1572864 | tf_op jit(solution)/shard_map/all_to_all | solution.py:184
  29.8 25.8 %collective-permute-start.12 = (bf16[48,1152]{1,0:T(8,128)(2,1)}, bf16[48,1152]{1,0:T(8,128)(2,1)S(1)}, u32[]{:S(2)}, u32[]{:S(2)}) collective-permute-start(bf16[48,1152]{1,0:T(8,128)(2,1)} %param.31), channel_id=1, source_target_pairs={{0,24},{8,0},{16,8},{24,16},{1,25},{9,1},{17,9},{25,17},{2,26},{10... | collective-permute-start | bytes 331784 | tf_op jit(solution)/shard_map/ppermute | solution.py:154
  93.9 24.0 %collective-permute-start.32 = (bf16[2,2,48,1536]{3,2,1,0:T(8,128)(2,1)}, bf16[2,2,48,1536]{3,2,1,0:T(8,128)(2,1)}, u32[]{:S(2)}, u32[]{:S(2)}) collective-permute-start(bf16[2,2,48,1536]{3,2,1,0:T(8,128)(2,1)} %get-tuple-element.83), channel_id=1, source_target_pairs={{0,4},{4,0},{1,5},{5,1},{2,6},{6,2},{3,7},{7,3},{8,12},{12,8},{9,1... | collective-permute-start | bytes 1769480 | tf_op jit(solution)/shard_map/ppermute | solution.py:154
  96.1 24.3 %collective-permute-start.27 = (bf16[2,2,48,1536]{3,2,1,0:T(8,128)(2,1)}, bf16[2,2,48,1536]{3,2,1,0:T(8,128)(2,1)}, u32[]{:S(2)}, u32[]{:S(2)}) collective-permute-start(bf16[2,2,48,1536]{3,2,1,0:T(8,128)(2,1)} %get-tuple-element.81), channel_id=1, source_target_pairs={{0,1},{1,0},{2,3},{3,2},{4,5},{5,4},{6,7},{7,6},{8,9},{9,8},{10,11... | collective-permute-start | bytes 1769480 | tf_op jit(solution)/shard_map/ppermute | solution.py:154
  97.3 39.5 %collective-permute-start.41 = (bf16[2,2,192,384]{3,2,1,0:T(8,128)(2,1)}, bf16[2,2,192,384]{3,2,1,0:T(8,128)(2,1)}, u32[]{:S(2)}, u32[]{:S(2)}) collective-permute-start(bf16[2,2,192,384]{3,2,1,0:T(8,128)(2,1)} %get-tuple-element.79), channel_id=1, source_target_pairs={{0,4},{4,0},{1,5},{5,1},{2,6},{6,2},{3,7},{7,3},{8,12},{12,8},{9,1... | collective-permute-start | bytes 1769480 | tf_op jit(solution)/shard_map/ppermute | solution.py:154
  102.6 37.0 %collective-permute-start.36 = (bf16[2,2,192,384]{3,2,1,0:T(8,128)(2,1)}, bf16[2,2,192,384]{3,2,1,0:T(8,128)(2,1)}, u32[]{:S(2)}, u32[]{:S(2)}) collective-permute-start(bf16[2,2,192,384]{3,2,1,0:T(8,128)(2,1)} %get-tuple-element.77), channel_id=1, source_target_pairs={{0,1},{1,0},{2,3},{3,2},{4,5},{5,4},{6,7},{7,6},{8,9},{9,8},{10,11... | collective-permute-start | bytes 1769480 | tf_op jit(solution)/shard_map/ppermute | solution.py:154
  106.4 42.3 %collective-permute-start.10 = (bf16[2,2,2,48,1152]{4,3,2,1,0:T(8,128)(2,1)}, bf16[2,2,2,48,1152]{4,3,2,1,0:T(8,128)(2,1)}, u32[]{:S(2)}, u32[]{:S(2)}) collective-permute-start(bf16[2,2,2,48,1152]{4,3,2,1,0:T(8,128)(2,1)} %get-tuple-element.73), channel_id=1, source_target_pairs={{0,2},{2,0},{1,3},{3,1},{4,6},{6,4},{5,7},{7,5},{8,10},{10,8},{9,1... | collective-permute-start | bytes 2654216 | tf_op jit(solution)/shard_map/ppermute | solution.py:154
  109.0 35.6 %all-to-all-start.2 = ((bf16[16,32,768]{2,1,0:T(8,128)(2,1)}), bf16[16,32,768]{2,1,0:T(8,128)(2,1)S(1)}, u32[]{:S(2)}, u32[]{:S(2)}) async-start(bf16[16,32,768]{2,1,0:T(8,128)(2,1)} %bitcast.529), calls=%async_computation.2 | async-start | bytes 1572864 | tf_op jit(solution)/shard_map/all_to_all | solution.py:185
  117.8 32.3 %collective-permute-start.15 = (bf16[2,2,2,48,1152]{4,3,2,1,0:T(8,128)(2,1)}, bf16[2,2,2,48,1152]{4,3,2,1,0:T(8,128)(2,1)}, u32[]{:S(2)}, u32[]{:S(2)}) collective-permute-start(bf16[2,2,2,48,1152]{4,3,2,1,0:T(8,128)(2,1)} %get-tuple-element.75), channel_id=1, source_target_pairs={{0,2},{2,0},{1,3},{3,1},{4,6},{6,4},{5,7},{7,5},{8,10},{10,8},{9,1... | collective-permute-start | bytes 2654216 | tf_op jit(solution)/shard_map/ppermute | solution.py:154
  120.5 70.3 %collective-permute-start.33 = (bf16[2,2,2,48,1536]{4,3,2,1,0:T(8,128)(2,1)}, bf16[2,2,2,48,1536]{4,3,2,1,0:T(8,128)(2,1)}, u32[]{:S(2)}, u32[]{:S(2)}) collective-permute-start(bf16[2,2,2,48,1536]{4,3,2,1,0:T(8,128)(2,1)} %get-tuple-element.71), channel_id=1, source_target_pairs={{0,2},{2,0},{1,3},{3,1},{4,6},{6,4},{5,7},{7,5},{8,10},{10,8},{9,1... | collective-permute-start | bytes 3538952 | tf_op jit(solution)/shard_map/ppermute | solution.py:154
  136.8 55.8 %collective-permute-start.28 = (bf16[2,2,2,48,1536]{4,3,2,1,0:T(8,128)(2,1)}, bf16[2,2,2,48,1536]{4,3,2,1,0:T(8,128)(2,1)}, u32[]{:S(2)}, u32[]{:S(2)}) collective-permute-start(bf16[2,2,2,48,1536]{4,3,2,1,0:T(8,128)(2,1)} %get-tuple-element.69), channel_id=1, source_target_pairs={{0,2},{2,0},{1,3},{3,1},{4,6},{6,4},{5,7},{7,5},{8,10},{10,8},{9,1... | collective-permute-start | bytes 3538952 | tf_op jit(solution)/shard_map/ppermute | solution.py:154
  139.6 86.3 %collective-permute-start.42 = (bf16[2,2,2,192,384]{4,3,2,1,0:T(8,128)(2,1)}, bf16[2,2,2,192,384]{4,3,2,1,0:T(8,128)(2,1)}, u32[]{:S(2)}, u32[]{:S(2)}) collective-permute-start(bf16[2,2,2,192,384]{4,3,2,1,0:T(8,128)(2,1)} %get-tuple-element.67), channel_id=1, source_target_pairs={{0,2},{2,0},{1,3},{3,1},{4,6},{6,4},{5,7},{7,5},{8,10},{10,8},{9,1... | collective-permute-start | bytes 3538952 | tf_op jit(solution)/shard_map/ppermute | solution.py:154
  148.8 79.1 %collective-permute-start.37 = (bf16[2,2,2,192,384]{4,3,2,1,0:T(8,128)(2,1)}, bf16[2,2,2,192,384]{4,3,2,1,0:T(8,128)(2,1)}, u32[]{:S(2)}, u32[]{:S(2)}) collective-permute-start(bf16[2,2,2,192,384]{4,3,2,1,0:T(8,128)(2,1)} %get-tuple-element.65), channel_id=1, source_target_pairs={{0,2},{2,0},{1,3},{3,1},{4,6},{6,4},{5,7},{7,5},{8,10},{10,8},{9,1... | collective-permute-start | bytes 3538952 | tf_op jit(solution)/shard_map/ppermute | solution.py:154
  334.6 108.9 %collective-permute-start.82 = (bf16[2,2,2,192,384]{4,3,2,1,0:T(8,128)(2,1)}, bf16[2,2,2,192,384]{4,3,2,1,0:T(8,128)(2,1)}, u32[]{:S(2)}, u32[]{:S(2)}) collective-permute-start(bf16[2,2,2,192,384]{4,3,2,1,0:T(8,128)(2,1)} %bitcast.196), channel_id=1, source_target_pairs={{0,2},{2,0},{1,3},{3,1},{4,6},{6,4},{5,7},{7,5},{8,10},{10,8},{9,1... | collective-permute-start | bytes 3538952 | tf_op jit(solution)/shard_map/ppermute | solution.py:161
  360.3 57.4 %collective-permute-start.64 = (bf16[2,2,2,48,384]{4,3,2,1,0:T(8,128)(2,1)}, bf16[2,2,2,48,384]{4,3,2,1,0:T(8,128)(2,1)}, u32[]{:S(2)}, u32[]{:S(2)}) collective-permute-start(bf16[2,2,2,48,384]{4,3,2,1,0:T(8,128)(2,1)} %bitcast.162), channel_id=1, source_target_pairs={{0,2},{2,0},{1,3},{3,1},{4,6},{6,4},{5,7},{7,5},{8,10},{10,8},{9,1... | collective-permute-start | bytes 884744 | tf_op jit(solution)/shard_map/ppermute | solution.py:161
  383.2 89.7 %all-to-all-start.3 = ((bf16[16,32,768]{2,1,0:T(8,128)(2,1)}), bf16[16,32,768]{2,1,0:T(8,128)(2,1)}, u32[]{:S(2)}, u32[]{:S(2)}) async-start(bf16[16,32,768]{2,1,0:T(8,128)(2,1)} %bitcast.126), calls=%async_computation.3 | async-start | bytes 1572864 | tf_op jit(solution)/shard_map/all_to_all | solution.py:309
  446.9 62.1 %collective-permute-start.83 = (bf16[2,2,192,384]{3,2,1,0:T(8,128)(2,1)}, bf16[2,2,192,384]{3,2,1,0:T(8,128)(2,1)}, u32[]{:S(2)}, u32[]{:S(2)}) collective-permute-start(bf16[2,2,192,384]{3,2,1,0:T(8,128)(2,1)} %fusion.46), channel_id=1, source_target_pairs={{0,4},{4,0},{1,5},{5,1},{2,6},{6,2},{3,7},{7,3},{8,12},{12,8},{9,1... | collective-permute-start | bytes 1769480 | tf_op jit(solution)/shard_map/ppermute | solution.py:161
  448.6 63.3 %collective-permute-start.79 = (bf16[2,2,192,384]{3,2,1,0:T(8,128)(2,1)}, bf16[2,2,192,384]{3,2,1,0:T(8,128)(2,1)}, u32[]{:S(2)}, u32[]{:S(2)}) collective-permute-start(bf16[2,2,192,384]{3,2,1,0:T(8,128)(2,1)} %fusion.45), channel_id=1, source_target_pairs={{0,1},{1,0},{2,3},{3,2},{4,5},{5,4},{6,7},{7,6},{8,9},{9,8},{10,11... | collective-permute-start | bytes 1769480 | tf_op jit(solution)/shard_map/ppermute | solution.py:161
  477.2 27.8 %collective-permute-start.58 = (bf16[48,1152]{1,0:T(8,128)(2,1)}, bf16[48,1152]{1,0:T(8,128)(2,1)S(1)}, u32[]{:S(2)}, u32[]{:S(2)}) collective-permute-start(bf16[48,1152]{1,0:T(8,128)(2,1)} %get-tuple-element.104), channel_id=1, source_target_pairs={{0,16},{8,24},{16,0},{24,8},{1,17},{9,25},{17,1},{25,9},{2,18},{10... | collective-permute-start | bytes 331784 | tf_op jit(solution)/shard_map/ppermute | solution.py:161
  479.9 26.6 %collective-permute-start.59 = (bf16[48,1152]{1,0:T(8,128)(2,1)S(1)}, bf16[48,1152]{1,0:T(8,128)(2,1)S(1)}, u32[]{:S(2)}, u32[]{:S(2)}) collective-permute-start(bf16[48,1152]{1,0:T(8,128)(2,1)S(1)} %get-tuple-element.105), channel_id=1, source_target_pairs={{0,8},{8,16},{16,24},{24,0},{1,9},{9,17},{17,25},{25,1},{2,10},{10... | collective-permute-start | bytes 331784 | tf_op jit(solution)/shard_map/ppermute | solution.py:161
  484.0 23.3 %collective-permute-start.54 = (bf16[48,1152]{1,0:T(8,128)(2,1)}, bf16[48,1152]{1,0:T(8,128)(2,1)}, u32[]{:S(2)}, u32[]{:S(2)}) collective-permute-start(bf16[48,1152]{1,0:T(8,128)(2,1)} %fusion.82), channel_id=1, source_target_pairs={{0,24},{8,0},{16,8},{24,16},{1,25},{9,1},{17,9},{25,17},{2,26},{10... | collective-permute-start | bytes 331784 | tf_op jit(solution)/shard_map/ppermute | solution.py:161
  (140 other events, 1492.8 us)
